TPU v7x, 32 devices: a whole 2x2x4 slice. The times are simulated.
32 devices in a mesh: dp: 4 (over z), bal: 4 (over x, core), tensor: 2 (over y).
Axes of the slice: x: 2, y: 2, z: 4, core: 2. Of those that a mesh axis runs over, the one named last changes fastest.
Arguments:
- tiles: bfloat16 [4, 4, 16, 1280, 128], P('dp', 'bal', None, 'tensor'), may hold values from -6 to 6
- tile_counts: int32 [4, 4], P('dp'), may hold values from 1 to 16, 32 in all within a row
- doc_order: int32 [4, 4], P('dp'), may hold values from 0 to 3, each once within a row
- qkv_weight: bfloat16 [3, 1280, 1280], P(None, 'dp', 'tensor'), may hold values from -6 to 6
- out_weight: bfloat16 [1280, 1280], P('dp', 'tensor'), may hold values from -0.625 to 0.625
Outputs:
- encoded: bfloat16 [4, 32, 1280, 128], P('dp', 'bal', 'tensor')
Inputs may be any that keep to these rules, and one draw needn't show every extreme that they name: `tile_counts`: each row sums to 32, and in every row some document has exactly 16 tiles. `doc_order`: each row names every document once.
All inputs are finite; a program needn't handle non-finite values.
Results may differ from a plain program's by a relative error of at most 0.012.
Values may be sent and summed in bfloat16 or wider, within the bound.
A program may use at most 64 MiB of HBM per device.

v0:
```python
import functools

import jax
import jax.numpy as jnp
from jax import lax
from jax.experimental import pallas as pl
from jax.experimental.pallas import tpu as pltpu
from jax.sharding import PartitionSpec as P

HDIM = 80
CAP = 8
CHUNK = 2
EPSILON = 1e-06
MESH = pl.DeviceIdType.MESH


def flip(index, bit):
    return index + bit - 2 * bit * ((index // bit) % 2)


def bits_of(size):
    bits = []
    while 1 << len(bits) < size:
        bits.append(1 << len(bits))
    return bits


def remote(src, dst, send, recv, **device):
    return pltpu.make_async_remote_copy(
        src_ref=src, dst_ref=dst, send_sem=send, recv_sem=recv, device_id=device, device_id_type=MESH
    )


def encode_kernel(sizes, *refs):
    nd, nb, nt = sizes
    bits = bits_of(nb)
    ns = len(bits)
    counts, order, tiles, wq_in, wo_in, out = refs[:6]
    sends, recvs = refs[6 : 6 + ns], refs[6 + ns : 6 + 2 * ns]
    gath, wq, wo, wide_o, normed, qkv, context, own, p_out, p_in = refs[6 + 2 * ns : 16 + 2 * ns]
    sems = refs[16 + 2 * ns :]
    t_send, t_recv, y_send, y_recv, w_send, w_recv, d_send, d_recv, p_send, p_recv = sems[:10]
    l_send, l_recv, h_send, h_recv = sems[10:]
    z, b, t = lax.axis_index("dp"), lax.axis_index("bal"), lax.axis_index("tensor")
    _, slices, patches = tiles.shape
    chunks = CAP // CHUNK

    barrier = pltpu.get_barrier_semaphore()
    for m in bits:
        pl.semaphore_signal(barrier, inc=1, device_id={"bal": flip(b, m)}, device_id_type=MESH)
    for j in range(1, nt):
        pl.semaphore_signal(barrier, inc=1, device_id={"tensor": (t + j) % nt}, device_id_type=MESH)

    def greet(j, carry):
        pl.semaphore_signal(barrier, inc=1, device_id={"dp": (z + j) % nd}, device_id_type=MESH)
        return carry

    lax.fori_loop(1, nd, greet, 0)
    pl.semaphore_wait(barrier, ns + nt - 1 + nd - 1)

    def spread(j):
        return remote(wo_in.at[b], wo.at[z, b], w_send.at[j], w_recv.at[j], dp=(z + j) % nd)

    part_count = wq.shape[2]
    part = b % part_count

    def line(way, s):
        step = 1 - 2 * way
        src = z - step * s
        there = z + step
        valid = (src >= 0) & (src < nd) & (there >= 0) & (there < nd)
        dst = wq.at[:, jnp.clip(src, 0, nd - 1), part]
        origin = wq_in.at[:, part] if isinstance(s, int) and s == 0 else dst
        copy = remote(
            origin, dst, l_send.at[way, s], l_recv.at[way, s], dp=jnp.clip(there, 0, nd - 1)
        )
        return valid, copy

    def arrival(way, s):
        step = 1 - 2 * way
        src = z - step * (s + 1)
        valid = (src >= 0) & (src < nd)
        at = wq.at[:, jnp.clip(src, 0, nd - 1), part]
        here = remote(
            at, at, l_send.at[way, s], l_recv.at[way, s], dp=jnp.clip(z + step, 0, nd - 1)
        )
        half = remote(at, at, h_send.at[way, s], h_recv.at[way, s], bal=flip(b, 1))
        return valid, here, half

    for way in range(2):
        valid, copy = line(way, 0)
        pl.when(valid)(copy.start)

    def hop(s):
        for way in range(2):
            valid, here, half = arrival(way, s)
            further, copy = line(way, s + 1)

            @pl.when(valid)
            def _(here=here, half=half, further=further, copy=copy):
                here.wait_recv()
                pl.when(further)(copy.start)
                if part_count > 1:
                    half.start()

    def tile_copy(s, slot, c):
        part = pl.ds(c * CHUNK, CHUNK)
        return remote(
            sends[s].at[slot, part],
            recvs[s].at[slot, part],
            t_send.at[s, slot, c],
            t_recv.at[s, slot, c],
            bal=flip(b, bits[s]),
        )

    def slot_of(s, r):
        return r >> (s + 1)

    def wait_for(s, r, c):
        for q in range(s):
            tile_copy(q, slot_of(q, r), c).wait_recv()

    docs = order.shape[1]
    placed = [order[0, p] for p in range(docs)]
    edges = [jnp.int32(0)]
    for doc in placed:
        edges.append(edges[-1] + counts[0, doc])
    own_start = jnp.int32(0)
    for p in range(docs):
        own_start = own_start + jnp.where(placed[p] == b, edges[p], 0)

    def current(s, r, i):
        block = b
        for m in bits:
            if r & m:
                block = flip(block, m)
        packed = block * CAP + i
        owner = jnp.int32(0)
        for p in range(docs):
            inside = (edges[p] <= packed) & (packed < edges[p + 1])
            owner = owner + jnp.where(inside, placed[p], 0)
        value = tiles[jnp.clip(packed - own_start, 0, tiles.shape[0] - 1)]
        for q in range(s):
            apart = (owner // bits[q]) % 2 != (b // bits[q]) % 2
            value = lax.select(apart, recvs[q][slot_of(q, r), i], value)
        return value

    for s, m in enumerate(bits):
        wanted = [r for r in range(nb) if r & (m - 1) == 0 and r & m]
        for r in reversed(wanted):
            slot = slot_of(s, r - m)
            for c in range(chunks):
                wait_for(s, r, c)

                def fill(i, carry, s=s, r=r, slot=slot):
                    sends[s][slot, i] = current(s, r, i)
                    return carry

                lax.fori_loop(c * CHUNK, (c + 1) * CHUNK, fill, 0)
                tile_copy(s, slot, c).start()

    mine = pl.ds(pl.multiple_of(t * slices, 16), slices)

    def y_copy(c, j):
        part = gath.at[pl.ds(c * CHUNK, CHUNK), mine, :]
        return remote(part, part, y_send.at[c, j], y_recv.at[c, j], tensor=(t + j) % nt)

    early = min((chunks + 1) // 2, nd - 2)
    for c in range(chunks):
        wait_for(ns, 0, c)

        def settle(i, carry):
            gath[i, mine, :] = current(ns, 0, i)
            return carry

        lax.fori_loop(c * CHUNK, (c + 1) * CHUNK, settle, 0)
        for j in range(1, nt):
            y_copy(c, j).start()
        if c % 2 == 0 and c // 2 < early:
            hop(c // 2)

    def start_spread(j, carry):
        spread(j).start()
        return carry

    lax.fori_loop(1, nd, start_spread, 0)
    wq[:, z] = wq_in[...]
    wo[z] = wo_in[...]

    def doubled(j, s, e):
        src = (z + nd - j) % nd
        held = b
        for q in range(s):
            if (e >> q) & 1:
                held = flip(held, bits[ns - 1 - q])
        dst = wo.at[src, held]
        at = (1 << s) - 1 + e
        return remote(
            dst, dst, d_send.at[j, at], d_recv.at[j, at], bal=flip(b, bits[ns - 1 - s])
        )

    def finish(s):
        def further(j, carry):
            if s == 0:
                spread(j).wait_recv()
            else:
                for e in range(1 << (s - 1)):
                    doubled(j, s - 1, e).wait_recv()
            if s < ns:
                for e in range(1 << s):
                    doubled(j, s, e).start()
            return carry

        lax.fori_loop(1, nd, further, 0)

    def normalize(i):
        values = gath[i].astype(jnp.float32)
        center = values - jnp.mean(values, axis=0, keepdims=True)
        spread_of = jnp.mean(center * center, axis=0, keepdims=True)
        normed[:, i * patches : (i + 1) * patches] = (
            center * lax.rsqrt(spread_of + EPSILON)
        ).astype(normed.dtype)

    for c in range(chunks):
        for j in range(1, nt):
            y_copy(c, j).wait_recv()
        for i in range(c * CHUNK, (c + 1) * CHUNK):
            normalize(i)

    def rest(s, carry):
        hop(s)
        return carry

    lax.fori_loop(early, nd - 1, rest, 0)
    finish(0)

    def halves(s, carry):
        for way in range(2):
            valid, _, half = arrival(way, s)
            pl.when(valid)(half.wait_recv)
        return carry

    if part_count > 1:
        lax.fori_loop(0, nd - 1, halves, 0)

    def project(c):
        pair = normed[:, pl.ds(pl.multiple_of(c * CHUNK * patches, patches), CHUNK * patches)]

        def one(k, carry):
            qkv[k] = lax.dot_general(
                wq[k].reshape(normed.shape[0], slices),
                pair,
                (((0,), (0,)), ((), ())),
                preferred_element_type=jnp.float32,
            ).astype(qkv.dtype)
            return carry

        lax.fori_loop(0, qkv.shape[0], one, 0)

    project(0)
    for s in range(1, ns + 1):
        finish(s)
    part_rows = wo.shape[2]
    for y in range(nd):
        for e in range(nb):
            start = (y * nb + e) * part_rows
            wide_o[start : start + part_rows] = wo[y, e]

    def p_copy(c, j):
        part = pl.ds(c * CHUNK, CHUNK)
        return remote(
            p_out.at[j - 1, part], p_in.at[j - 1, part], p_send.at[c, j], p_recv.at[c, j],
            tensor=(t + j) % nt,
        )

    heads = slices // HDIM

    def partial(target):
        block = wide_o[pl.ds(pl.multiple_of(target * slices, 16), slices), :]
        return jnp.dot(block, context[...], preferred_element_type=jnp.float32).astype(own.dtype)

    def encode(c, carry):
        for i in range(CHUNK):
            here = slice(i * patches, (i + 1) * patches)
            for h in range(heads):
                span = slice(h * HDIM, (h + 1) * HDIM)
                scores = lax.dot_general(
                    qkv[1, span, here], qkv[0, span, here], (((0,), (0,)), ((), ())),
                    preferred_element_type=jnp.float32,
                ) * HDIM ** (-0.5)
                powers = jnp.exp(scores - jnp.max(scores, axis=0, keepdims=True))
                probs = powers * (1.0 / jnp.sum(powers, axis=0, keepdims=True))
                context[span, i * patches : (i + 1) * patches] = jnp.dot(
                    qkv[2, span, here], probs.astype(qkv.dtype), preferred_element_type=jnp.float32
                ).astype(context.dtype)
        for j in range(1, nt):
            block = partial((t + j) % nt)
            for i in range(CHUNK):
                p_out[j - 1, c * CHUNK + i] = block[:, i * patches : (i + 1) * patches]
            p_copy(c, j).start()
        block = partial(t)
        for i in range(CHUNK):
            own[c * CHUNK + i] = block[:, i * patches : (i + 1) * patches]

        @pl.when(c + 1 < chunks)
        def _():
            project(c + 1)

        return carry

    lax.fori_loop(0, chunks, encode, 0)

    def close(c, carry):
        for j in range(1, nt):
            p_copy(c, j).wait_recv()
        for i in range(CHUNK):
            at = c * CHUNK + i
            total = gath[at, mine, :].astype(jnp.float32) + own[at].astype(jnp.float32)
            for j in range(1, nt):
                total = total + p_in[j - 1, at].astype(jnp.float32)
            out[at] = total.astype(out.dtype)
        return carry

    lax.fori_loop(0, chunks, close, 0)

    for c in range(chunks):
        for j in range(1, nt):
            y_copy(c, j).wait_send()
            p_copy(c, j).wait_send()
    for s, m in enumerate(bits):
        for slot in range(nb >> (s + 1)):
            for c in range(chunks):
                tile_copy(s, slot, c).wait_send()
    def drain(j, carry):
        spread(j).wait_send()
        for s in range(ns):
            for e in range(1 << s):
                doubled(j, s, e).wait_send()
        return carry

    lax.fori_loop(1, nd, drain, 0)

    def drain_line(s, carry):
        for way in range(2):
            valid, copy = line(way, s)
            pl.when(valid)(copy.wait_send)
            valid, _, half = arrival(way, s)
            if part_count > 1:
                pl.when(valid)(half.wait_send)
        return carry

    lax.fori_loop(0, nd - 1, drain_line, 0)


def encode_all(counts, ordering, tiles, qkv_weight, out_weight):
    nd, nb, nt = (lax.axis_size(name) for name in ("dp", "bal", "tensor"))
    ns = len(bits_of(nb))
    slots, slices, patches = tiles.shape
    kinds, rows, columns = qkv_weight.shape
    wq = qkv_weight.reshape(kinds, min(nb, 2), -1, columns)
    wo = out_weight.reshape(nb, -1, columns)
    chunks = CAP // CHUNK
    dtype = tiles.dtype
    vmem = pl.BlockSpec(memory_space=pltpu.VMEM)
    dma = pltpu.SemaphoreType.DMA

    def space(*shape):
        return pltpu.VMEM(shape, dtype)

    buffers = [space(nb >> (s + 1), CAP, slices, patches) for s in range(ns)]
    return pl.pallas_call(
        functools.partial(encode_kernel, (nd, nb, nt)),
        out_shape=jax.ShapeDtypeStruct((CAP, slices, patches), dtype),
        in_specs=[pl.BlockSpec(memory_space=pltpu.SMEM)] * 2 + [vmem] * 3,
        out_specs=vmem,
        scratch_shapes=buffers
        + buffers
        + [
            space(CAP, nt * slices, patches),
            space(kinds, nd, *wq.shape[1:]),
            space(nd, *wo.shape),
            space(nt * slices, columns),
            space(nt * slices, CAP * patches),
            space(kinds, columns, CHUNK * patches),
            space(columns, CHUNK * patches),
            space(CAP, slices, patches),
            space(max(nt - 1, 1), CAP, slices, patches),
            space(max(nt - 1, 1), CAP, slices, patches),
        ]
        + [dma((ns, max(nb // 2, 1), chunks))] * 2
        + [dma((chunks, nt))] * 2
        + [dma((nd,))] * 2
        + [dma((nd, nb))] * 2
        + [dma((chunks, nt))] * 2
        + [dma((2, nd))] * 4,
        compiler_params=pltpu.CompilerParams(
            collective_id=0, has_side_effects=True, vmem_limit_bytes=60 * 1024 * 1024
        ),
        name="encode_all",
    )(counts, ordering, tiles, wq, wo)


def local(tiles, tile_counts, doc_order, qkv_weight, out_weight):
    own_tiles = tiles[0, 0]
    return encode_all(tile_counts, doc_order, own_tiles, qkv_weight, out_weight)[None]


def solution(mesh):
    placed = (
        P("dp", "bal", None, "tensor", None),
        P("dp", None),
        P("dp", None),
        P(None, "dp", "tensor"),
        P("dp", "tensor"),
    )
    return jax.shard_map(
        local, mesh=mesh, in_specs=placed, out_specs=P("dp", "bal", "tensor", None), check_vma=False
    )
```

profile of v0, /device:TPU:0, one launch (start us, length us, event | category | flops | bytes accessed | tf_op | source)
XLA Modules:
  0.0 98.7 jit_solution(3782083491252440936)
XLA Ops:
  0.0 96.3 %encode_all.1 = bf16[8,640,128]{2,1,0:T(8,128)(2,1)} custom-call(s32[1,4]{1,0:T(1,128)} %refs_0_.1, s32[1,4]{1,0:T(1,128)} %refs_1_.1, bf16[16,640,128]{2,1,0:T(8,128)(2,1)} %bitcast.5, bf16[3,2,160,640]{3,2,1,0:T(8,128)(2,1)} %bitcast.6, bf16[4,80,640]{2,1,0:T(8,128)(2,1)} %bitcast.7), custom_call_target="tpu_custom_call" | custom-call | tf_op jit(solution)/shard_map/encode_all/pallas_call | solution.py:371
  96.3 2.5 %copy.7 = bf16[1,8,640,128]{3,2,1,0:T(8,128)(2,1)} copy(bf16[1,8,640,128]{3,2,1,0:T(8,128)(2,1)} %bitcast.4) | data formatting | bytes 2621440
where the time goes:
time: 99 us; the launch traced here: 98.7 us
  Pallas kernels  96.3 us (97%)
  local copies, waits for them, and re-layouts  2.47 us (2%)
    pallas_call x1, Pallas kernels, encode_all(): pl.pallas_call(functools.partial(encode_kernel, (nd, nb, nt)), out_shape=...  96.3 us
    unnamed x1, local copies, waits for them, and re-layouts  2.47 us

commit v1 on v0

v1 whole, which is shorter than its diff:
```python
import functools

import jax
import jax.numpy as jnp
from jax import lax
from jax.experimental import pallas as pl
from jax.experimental.pallas import tpu as pltpu
from jax.sharding import PartitionSpec as P

HDIM = 80
CAP = 8
LANES = 128
GROUP = 4
EPSILON = 1e-06
LOG2E = 1.4426950408889634
MESH = pl.DeviceIdType.MESH


def flip(index, bit):
    return index + bit - 2 * bit * ((index // bit) % 2)


def bits_of(size):
    bits = []
    while 1 << len(bits) < size:
        bits.append(1 << len(bits))
    return bits


def column_groups(slices):
    width = LANES if slices % LANES == 0 else slices
    return width, slices // width


def pieces_of(slices):
    half = slices // 2
    first = [(0, 0, half), (0, half, half)] if half % 16 == 0 else [(0, 0, slices)]
    return first + [(i, 0, slices) for i in range(1, CAP)]


def remote(src, dst, send, recv, **device):
    return pltpu.make_async_remote_copy(
        src_ref=src, dst_ref=dst, send_sem=send, recv_sem=recv, device_id=device, device_id_type=MESH
    )


def encode_kernel(sizes, *refs):
    nd, nb, nt = sizes
    bits = bits_of(nb)
    ns = len(bits)
    counts, order, tiles_in, wq_in, wo_in, out = refs[:6]
    sends, recvs = refs[6 : 6 + ns], refs[6 + ns : 6 + 2 * ns]
    tiles, gath, wq, wt, wo_own, wo, normed, qkv, ctx, own = refs[6 + 2 * ns : 16 + 2 * ns]
    sems = refs[16 + 2 * ns :]
    t_send, t_recv, y_send, y_recv, c_send, c_recv = sems[:6]
    l_send, l_recv, h_send, h_recv = sems[6:10]
    x_send, x_recv, w_send, w_recv, d_send, d_recv, i_sem = sems[10:]
    z, b, t = lax.axis_index("dp"), lax.axis_index("bal"), lax.axis_index("tensor")
    _, slices, patches = tiles.shape
    width, groups = column_groups(slices)
    pieces = pieces_of(slices)
    per = nd // nt
    features = nt * slices
    kinds = wq.shape[0]
    blocks = CAP // GROUP

    load_tiles = pltpu.make_async_copy(tiles_in, tiles, i_sem.at[0])
    load_q = pltpu.make_async_copy(wq_in, wq.at[:, z], i_sem.at[1])
    load_o = pltpu.make_async_copy(wo_in, wo_own, i_sem.at[2])
    load_tiles.start()
    load_q.start()
    load_o.start()

    barrier = pltpu.get_barrier_semaphore()
    for m in bits:
        pl.semaphore_signal(barrier, inc=1, device_id={"bal": flip(b, m)}, device_id_type=MESH)
    for j in range(1, nt):
        pl.semaphore_signal(barrier, inc=1, device_id={"tensor": (t + j) % nt}, device_id_type=MESH)

    def greet(j, carry):
        pl.semaphore_signal(barrier, inc=1, device_id={"dp": (z + j) % nd}, device_id_type=MESH)
        return carry

    lax.fori_loop(1, nd, greet, 0)

    docs = order.shape[1]
    placed = [order[0, p] for p in range(docs)]
    edges = [jnp.int32(0)]
    for doc in placed:
        edges.append(edges[-1] + counts[0, doc])
    own_start = jnp.int32(0)
    for p in range(docs):
        own_start = own_start + jnp.where(placed[p] == b, edges[p], 0)

    def slot_of(s, r):
        return r >> (s + 1)

    def current(s, r, i, rows):
        block = b
        for m in bits:
            if r & m:
                block = flip(block, m)
        packed = block * CAP + i
        owner = jnp.int32(0)
        for p in range(docs):
            inside = (edges[p] <= packed) & (packed < edges[p + 1])
            owner = owner + jnp.where(inside, placed[p], 0)
        value = tiles[jnp.clip(packed - own_start, 0, tiles.shape[0] - 1), rows]
        for q in range(s):
            apart = (owner // bits[q]) % 2 != (b // bits[q]) % 2
            value = lax.select(apart, recvs[q][slot_of(q, r), i, rows], value)
        return value

    def tile_copy(s, slot, p):
        i, start, count = pieces[p]
        rows = pl.ds(start, count)
        return remote(
            sends[s].at[slot, i, rows],
            recvs[s].at[slot, i, rows],
            t_send.at[s, slot, p],
            t_recv.at[s, slot, p],
            bal=flip(b, bits[s]),
        )

    def wait_for(s, r, p):
        for q in range(s):
            tile_copy(q, slot_of(q, r), p).wait_recv()

    def wanted(s):
        m = bits[s]
        return [r for r in reversed(range(nb)) if r & (m - 1) == 0 and r & m]

    load_tiles.wait()
    for r in wanted(0):
        slot = slot_of(0, r - 1)

        def fill(i, carry, r=r, slot=slot):
            sends[0][slot, i] = current(0, r, i, slice(None))
            return carry

        lax.fori_loop(0, CAP, fill, 0)

    load_o.wait()
    load_q.wait()
    keeper = z // per
    place = z % per

    @pl.when(keeper == t)
    def _():
        wo[t, place, b] = wo_own[b]

    pl.semaphore_wait(barrier, ns + nt - 1 + nd - 1)

    for r in wanted(0):
        for p in range(len(pieces)):
            tile_copy(0, slot_of(0, r - 1), p).start()

    part_count = wq.shape[2]
    part = b % part_count

    def held(src, k):
        return wq.at[:, jnp.clip(src, 0, nd - 1), part, :, pl.ds(k * width, width)]

    def line(way, s, k):
        step = 1 - 2 * way
        src = z - step * s
        there = z + step
        valid = (src >= 0) & (src < nd) & (there >= 0) & (there < nd)
        at = held(src, k)
        copy = remote(
            at, at, l_send.at[way, s, k], l_recv.at[way, s, k], dp=jnp.clip(there, 0, nd - 1)
        )
        return valid, copy

    def arrival(way, s, k):
        step = 1 - 2 * way
        src = z - step * (s + 1)
        valid = (src >= 0) & (src < nd)
        at = held(src, k)
        here = remote(
            at, at, l_send.at[way, s, k], l_recv.at[way, s, k], dp=jnp.clip(z + step, 0, nd - 1)
        )
        half = remote(at, at, h_send.at[way, s, k], h_recv.at[way, s, k], bal=flip(b, 1))
        return valid, here, half

    for k in range(groups):
        for way in range(2):
            valid, copy = line(way, 0, k)
            pl.when(valid)(copy.start)

    def hop(s, k):
        for way in range(2):
            valid, here, half = arrival(way, s, k)
            further, copy = line(way, s + 1, k)

            @pl.when(valid)
            def _(here=here, half=half, further=further, copy=copy):
                here.wait_recv()
                pl.when(further)(copy.start)
                if part_count > 1:
                    half.start()

    def halves(s, k):
        for way in range(2):
            valid, _, half = arrival(way, s, k)
            if part_count > 1:
                pl.when(valid)(half.wait_recv)

    def cross(source, target):
        return remote(
            wo_own.at[b], wo.at[source, place, b], x_send.at[0], x_recv.at[source], tensor=target
        )

    @pl.when(keeper != t)
    def _():
        cross(t, keeper).start()

    def spread(j):
        at = wo.at[:, place, b]
        return remote(at, at, w_send.at[j], w_recv.at[place], dp=(z + j) % nd)

    def spread_out():
        @pl.when(keeper == t)
        def _():
            for j in range(1, nt):
                cross((t + j) % nt, t).wait_recv()

            def start(j, carry):
                spread(j).start()
                return carry

            lax.fori_loop(1, nd, start, 0)

    def doubled(q, s, e):
        at = b
        for bit in range(s):
            if (e >> bit) & 1:
                at = flip(at, bits[ns - 1 - bit])
        rows = wo.at[:, q, at]
        index = (1 << s) - 1 + e
        return remote(
            rows, rows, d_send.at[q, index], d_recv.at[q, index], bal=flip(b, bits[ns - 1 - s])
        )

    def gathered(q):
        at = wo.at[:, q, b]
        return remote(at, at, w_send.at[0], w_recv.at[q], dp=(z + 1) % nd)

    def finish(s):
        def further(q, carry):
            if s == 0:
                pl.when(t * per + q != z)(gathered(q).wait_recv)
            else:
                for e in range(1 << (s - 1)):
                    doubled(q, s - 1, e).wait_recv()
            if s < ns:
                for e in range(1 << s):
                    doubled(q, s, e).start()
            return carry

        lax.fori_loop(0, per, further, 0)

    for s in range(1, ns):
        for r in wanted(s):
            slot = slot_of(s, r - bits[s])
            for p, (i, start, count) in enumerate(pieces):
                wait_for(s, r, p)
                rows = pl.ds(start, count)
                sends[s][slot, i, rows] = current(s, r, i, rows)
                tile_copy(s, slot, p).start()

    def y_copy(p, j):
        i, start, count = pieces[p]
        at = gath.at[i, pl.ds(pl.multiple_of(t * slices + start, 16), count), :]
        return remote(at, at, y_send.at[p, j], y_recv.at[p, j], tensor=(t + j) % nt)

    def normalize(i):
        for p, piece in enumerate(pieces):
            if piece[0] == i:
                for j in range(1, nt):
                    y_copy(p, j).wait_recv()
        values = gath[i].astype(jnp.float32)
        center = values - jnp.mean(values, axis=0, keepdims=True)
        spread_of = jnp.mean(center * center, axis=0, keepdims=True)
        normed[:, i * patches : (i + 1) * patches] = (
            center * lax.rsqrt(spread_of + EPSILON)
        ).astype(normed.dtype)

    early = min(2, nd - 1)
    forwards = [(s, k) for s in range(early) for k in range(groups)]
    slots = [1, 1, 2, 2, 3, 4, 5, 5, 6, 7]
    after = {}
    for n, pair in enumerate(forwards):
        after.setdefault(slots[n] if len(forwards) == len(slots) else CAP - 1, []).append(pair)
    for p, (i, start, count) in enumerate(pieces):
        wait_for(ns, 0, p)
        rows = pl.ds(start, count)
        gath[i, pl.ds(pl.multiple_of(t * slices + start, 16), count), :] = current(ns, 0, i, rows)
        for j in range(1, nt):
            y_copy(p, j).start()
        if start + count == slices:
            for s, k in after.get(i, []):
                hop(s, k)
            if i == 5:
                spread_out()
            if i >= 2:
                normalize(i - 2)

    def rest(k):
        def one(s, carry):
            hop(s, k)
            return carry

        lax.fori_loop(early, nd - 1, one, 0)

    def ready(k):
        def one(s, carry):
            halves(s, k)
            return carry

        lax.fori_loop(0, nd - 1, one, 0)
        for kind in range(kinds):
            block = wq[kind, :, :, :, k * width : (k + 1) * width].reshape(features, width)
            wt[kind * width : (kind + 1) * width, :] = block.T

    def heads_of(k):
        return [h for h in range(slices // HDIM) if k * width < (h + 1) * HDIM <= (k + 1) * width]

    def c_copy(k, g, j):
        first, number = heads_of(k)[0], len(heads_of(k))
        at = ctx.at[
            pl.ds(pl.multiple_of(t * slices + first * HDIM, 16), number * HDIM),
            pl.ds(pl.multiple_of(g * GROUP * patches, patches), GROUP * patches),
        ]
        return remote(at, at, c_send.at[k, g, j], c_recv.at[k, g, j], tensor=(t + j) % nt)

    def columns(i, number):
        return pl.ds(pl.multiple_of(i * patches, patches), number * patches)

    scale = HDIM ** (-0.5) * LOG2E

    def encode(k, g):
        for n in range(0, GROUP, 2):
            cols = columns(g * GROUP + n, 2)
            result = jnp.dot(wt[...], normed[:, cols], preferred_element_type=jnp.float32)
            for kind in range(kinds):
                qkv[kind, k * width : (k + 1) * width, cols] = result[
                    kind * width : (kind + 1) * width
                ].astype(qkv.dtype)
        for n in range(GROUP):
            cols = columns(g * GROUP + n, 1)
            for h in heads_of(k):
                span = slice(h * HDIM, (h + 1) * HDIM)
                scores = lax.dot_general(
                    qkv[1, span, cols], qkv[0, span, cols], (((0,), (0,)), ((), ())),
                    preferred_element_type=jnp.float32,
                )
                powers = jnp.exp2((scores - jnp.max(scores, axis=0, keepdims=True)) * scale)
                total = jnp.sum(powers, axis=0, keepdims=True)
                value = jnp.dot(
                    qkv[2, span, cols], powers.astype(qkv.dtype), preferred_element_type=jnp.float32
                )
                ctx[pl.ds(pl.multiple_of(t * slices + h * HDIM, 16), HDIM), cols] = (
                    value * (1.0 / total)
                ).astype(ctx.dtype)
        for j in range(1, nt):
            c_copy(k, g, j).start()

    rest(0)
    ready(0)
    encode(0, 0)
    if groups > 1:
        rest(1)
    for i in range(CAP - 2, CAP):
        normalize(i)

    def others(k, low):
        def one(g, carry):
            encode(k, g)
            return carry

        lax.fori_loop(low, blocks, one, 0)

    others(0, 1)
    for k in range(1, groups):
        ready(k)
        others(k, 0)
        if k + 1 < groups:
            rest(k + 1)
        if k <= ns:
            finish(k - 1)
    for s in range(min(groups - 1, ns), ns + 1):
        finish(s)

    def partial(source, cols):
        weight = wo[source].reshape(slices, slices)
        block = ctx[pl.ds(pl.multiple_of(source * slices, 16), slices), cols]
        return jnp.dot(weight, block, preferred_element_type=jnp.float32).astype(own.dtype)

    def mine(n, carry):
        own[:, columns(2 * n, 2)] = partial(t, columns(2 * n, 2))
        return carry

    lax.fori_loop(0, CAP // 2, mine, 0)

    def close(g, carry):
        for k in range(groups):
            for j in range(1, nt):
                c_copy(k, g, j).wait_recv()
        for n in range(0, GROUP, 2):
            i = g * GROUP + n
            total = own[:, columns(i, 2)].astype(jnp.float32)
            for j in range(1, nt):
                total = total + partial((t + j) % nt, columns(i, 2)).astype(jnp.float32)
            for e in range(2):
                source = gath[i + e, pl.ds(pl.multiple_of(t * slices, 16), slices), :]
                out[i + e] = (
                    source.astype(jnp.float32) + total[:, e * patches : (e + 1) * patches]
                ).astype(out.dtype)
        return carry

    lax.fori_loop(0, blocks, close, 0)

    for p in range(len(pieces)):
        for j in range(1, nt):
            y_copy(p, j).wait_send()
        for s in range(ns):
            for slot in range(nb >> (s + 1)):
                tile_copy(s, slot, p).wait_send()
    for k in range(groups):
        for j in range(1, nt):
            for g in range(blocks):
                c_copy(k, g, j).wait_send()

    @pl.when(keeper != t)
    def _():
        cross(t, keeper).wait_send()

    @pl.when(keeper == t)
    def _():
        def drain(j, carry):
            spread(j).wait_send()
            return carry

        lax.fori_loop(1, nd, drain, 0)

    def drain_doubled(q, carry):
        for s in range(ns):
            for e in range(1 << s):
                doubled(q, s, e).wait_send()
        return carry

    lax.fori_loop(0, per, drain_doubled, 0)

    def drain_line(s, carry):
        for k in range(groups):
            for way in range(2):
                valid, copy = line(way, s, k)
                pl.when(valid)(copy.wait_send)
                valid, _, half = arrival(way, s, k)
                if part_count > 1:
                    pl.when(valid)(half.wait_send)
        return carry

    lax.fori_loop(0, nd - 1, drain_line, 0)


def encode_all(counts, ordering, tiles, qkv_weight, out_weight):
    nd, nb, nt = (lax.axis_size(name) for name in ("dp", "bal", "tensor"))
    ns = len(bits_of(nb))
    slots, slices, patches = tiles.shape
    kinds, rows, columns = qkv_weight.shape
    width, groups = column_groups(columns)
    pieces = len(pieces_of(slices))
    per = nd // nt
    wq = qkv_weight.reshape(kinds, min(nb, 2), -1, columns)
    wo = out_weight.reshape(nb, -1, columns)
    dtype = tiles.dtype
    vmem = pl.BlockSpec(memory_space=pltpu.VMEM)
    hbm = pl.BlockSpec(memory_space=pltpu.HBM)
    dma = pltpu.SemaphoreType.DMA
    blocks = CAP // GROUP

    def space(*shape):
        return pltpu.VMEM(shape, dtype)

    buffers = [space(nb >> (s + 1), CAP, slices, patches) for s in range(ns)]
    return pl.pallas_call(
        functools.partial(encode_kernel, (nd, nb, nt)),
        out_shape=jax.ShapeDtypeStruct((CAP, slices, patches), dtype),
        in_specs=[pl.BlockSpec(memory_space=pltpu.SMEM)] * 2 + [hbm] * 3,
        out_specs=vmem,
        scratch_shapes=buffers
        + buffers
        + [
            space(slots, slices, patches),
            space(CAP, nt * slices, patches),
            space(kinds, nd, *wq.shape[1:]),
            space(kinds * width, nt * slices),
            space(*wo.shape),
            space(nt, per, *wo.shape),
            space(nt * slices, CAP * patches),
            space(kinds, columns, CAP * patches),
            space(nt * slices, CAP * patches),
            space(slices, CAP * patches),
        ]
        + [dma((ns, max(nb // 2, 1), pieces))] * 2
        + [dma((pieces, nt))] * 2
        + [dma((groups, blocks, nt))] * 2
        + [dma((2, nd, groups))] * 4
        + [dma((1,)), dma((nt,)), dma((nd,)), dma((per,))]
        + [dma((per, nb))] * 2
        + [dma((3,))],
        compiler_params=pltpu.CompilerParams(
            collective_id=0, has_side_effects=True, vmem_limit_bytes=44 * 1024 * 1024
        ),
        name="encode_all",
    )(counts, ordering, tiles, wq, wo)


def local(tiles, tile_counts, doc_order, qkv_weight, out_weight):
    own_tiles = tiles[0, 0]
    return encode_all(tile_counts, doc_order, own_tiles, qkv_weight, out_weight)[None]


def solution(mesh):
    placed = (
        P("dp", "bal", None, "tensor", None),
        P("dp", None),
        P("dp", None),
        P(None, "dp", "tensor"),
        P("dp", "tensor"),
    )
    return jax.shard_map(
        local, mesh=mesh, in_specs=placed, out_specs=P("dp", "bal", "tensor", None), check_vma=False
    )
```

time: 99 us -> 92.2 us (0.931)
  Pallas kernels: 96.3 us -> 85.5 us
  local copies, waits for them, and re-layouts: 2.47 us -> 6.4 us
    pallas_call x1, Pallas kernels: 96.3 us -> 85.5 us  [encode_all(): pl.pallas_call(functools.partial(encode_kernel, (nd, nb, nt)), out_shape=...]
    unnamed x1 -> x11, local copies, waits for them, and re-layouts: 2.47 us -> 6.4 us
where the time goes in v1:
time: 92.2 us; the launch traced here: 92 us
  Pallas kernels  85.5 us (93%)
  local copies, waits for them, and re-layouts  6.4 us (7%)
    pallas_call x1, Pallas kernels, encode_all(): pl.pallas_call(functools.partial(encode_kernel, (nd, nb, nt)), out_shape=...  85.5 us
    unnamed x11, local copies, waits for them, and re-layouts  6.4 us

profile of v1, /device:TPU:0, one launch (start us, length us, event | category | flops | bytes accessed | tf_op | source)
XLA Modules:
  0.0 92.0 jit_solution(9866191453839027914)
XLA Ops:
  0.0 0.0 copy-start
  0.0 1.7 %copy-done = bf16[1,1,16,640,128]{4,3,2,1,0:T(8,128)(2,1)S(1)} copy-done((bf16[1,1,16,640,128]{4,3,2,1,0:T(8,128)(2,1)S(1)}, bf16[1,1,16,640,128]{4,3,2,1,0:T(8,128)(2,1)}, u32[]{:S(2)}) %copy-start) | copy-done | bytes 2621464
  1.7 0.0 copy-start.1
  1.7 1.3 %copy-done.1 = bf16[3,320,640]{2,1,0:T(8,128)(2,1)S(1)} copy-done((bf16[3,320,640]{2,1,0:T(8,128)(2,1)S(1)}, bf16[3,320,640]{2,1,0:T(8,128)(2,1)}, u32[]{:S(2)}) %copy-start.1) | copy-done | bytes 1228824
  3.0 0.0 copy-start.2
  3.0 1.0 %copy-done.2 = bf16[320,640]{1,0:T(8,128)(2,1)S(1)} copy-done((bf16[320,640]{1,0:T(8,128)(2,1)S(1)}, bf16[320,640]{1,0:T(8,128)(2,1)}, u32[]{:S(2)}) %copy-start.2) | copy-done | bytes 409624
  4.0 0.0 copy-start.3
  4.0 0.7 copy-done.3
  4.7 0.0 copy-start.4
  4.7 0.7 copy-done.4
  5.3 85.5 %encode_all.1 = bf16[8,640,128]{2,1,0:T(8,128)(2,1)S(1)} custom-call(s32[1,4]{1,0:T(1,128)S(1)} %copy-done.3, s32[1,4]{1,0:T(1,128)S(1)} %copy-done.4, bf16[16,640,128]{2,1,0:T(8,128)(2,1)S(1)} %bitcast.5, bf16[3,2,160,640]{3,2,1,0:T(8,128)(2,1)S(1)} %bitcast.6, bf16[4,80,640]{2,1,0:T(8,128)(2,1)S(1)} %bitcast.7), custom_call_target="tpu_custom_call" | custom-call | tf_op jit(solution)/shard_map/encode_all/pallas_call | solution.py:488
  90.9 1.1 %copy.7 = bf16[1,8,640,128]{3,2,1,0:T(8,128)(2,1)} copy(bf16[1,8,640,128]{3,2,1,0:T(8,128)(2,1)S(1)} %bitcast.4) | data formatting | bytes 2621440
Async XLA Ops:
  0.0 1.7 %copy-start = (bf16[1,1,16,640,128]{4,3,2,1,0:T(8,128)(2,1)S(1)}, bf16[1,1,16,640,128]{4,3,2,1,0:T(8,128)(2,1)}, u32[]{:S(2)}) copy-start(bf16[1,1,16,640,128]{4,3,2,1,0:T(8,128)(2,1)} %param.5) | copy-start | bytes 7864324
  1.7 1.3 %copy-start.1 = (bf16[3,320,640]{2,1,0:T(8,128)(2,1)S(1)}, bf16[3,320,640]{2,1,0:T(8,128)(2,1)}, u32[]{:S(2)}) copy-start(bf16[3,320,640]{2,1,0:T(8,128)(2,1)} %param.8) | copy-start | bytes 3686404
  3.0 1.0 %copy-start.2 = (bf16[320,640]{1,0:T(8,128)(2,1)S(1)}, bf16[320,640]{1,0:T(8,128)(2,1)}, u32[]{:S(2)}) copy-start(bf16[320,640]{1,0:T(8,128)(2,1)} %param.9) | copy-start | bytes 1228804
  4.0 0.7 copy-start.3
  4.7 0.7 copy-start.4

commit v2 on v1

--- a/solution.py
+++ b/solution.py
@@ -11,6 +11,7 @@
 CAP = 8
 LANES = 128
 GROUP = 4
+PAIR = 2
 EPSILON = 1e-06
 LOG2E = 1.4426950408889634
 MESH = pl.DeviceIdType.MESH
@@ -54,7 +55,7 @@
     sems = refs[16 + 2 * ns :]
     t_send, t_recv, y_send, y_recv, c_send, c_recv = sems[:6]
     l_send, l_recv, h_send, h_recv = sems[6:10]
-    x_send, x_recv, w_send, w_recv, d_send, d_recv, i_sem = sems[10:]
+    x_send, x_recv, d_send, d_recv, i_sem = sems[10:]
     z, b, t = lax.axis_index("dp"), lax.axis_index("bal"), lax.axis_index("tensor")
     _, slices, patches = tiles.shape
     width, groups = column_groups(slices)
@@ -159,77 +160,24 @@
     part = b % part_count
 
     def held(src, k):
-        return wq.at[:, jnp.clip(src, 0, nd - 1), part, :, pl.ds(k * width, width)]
+        src = jnp.clip(src, 0, nd - 1)
+        if k == groups:
+            return wo.at[:, src % per, b]
+        return wq.at[:, src, part, :, pl.ds(k * width, width)]
+
+    def exists(src, k):
+        valid = (src >= 0) & (src < nd)
+        return valid & (src // per == t) if k == groups else valid
 
     def line(way, s, k):
         step = 1 - 2 * way
         src = z - step * s
         there = z + step
-        valid = (src >= 0) & (src < nd) & (there >= 0) & (there < nd)
         at = held(src, k)
         copy = remote(
             at, at, l_send.at[way, s, k], l_recv.at[way, s, k], dp=jnp.clip(there, 0, nd - 1)
         )
-        return valid, copy
-
-    def arrival(way, s, k):
-        step = 1 - 2 * way
-        src = z - step * (s + 1)
-        valid = (src >= 0) & (src < nd)
-        at = held(src, k)
-        here = remote(
-            at, at, l_send.at[way, s, k], l_recv.at[way, s, k], dp=jnp.clip(z + step, 0, nd - 1)
-        )
-        half = remote(at, at, h_send.at[way, s, k], h_recv.at[way, s, k], bal=flip(b, 1))
-        return valid, here, half
-
-    for k in range(groups):
-        for way in range(2):
-            valid, copy = line(way, 0, k)
-            pl.when(valid)(copy.start)
-
-    def hop(s, k):
-        for way in range(2):
-            valid, here, half = arrival(way, s, k)
-            further, copy = line(way, s + 1, k)
-
-            @pl.when(valid)
-            def _(here=here, half=half, further=further, copy=copy):
-                here.wait_recv()
-                pl.when(further)(copy.start)
-                if part_count > 1:
-                    half.start()
-
-    def halves(s, k):
-        for way in range(2):
-            valid, _, half = arrival(way, s, k)
-            if part_count > 1:
-                pl.when(valid)(half.wait_recv)
-
-    def cross(source, target):
-        return remote(
-            wo_own.at[b], wo.at[source, place, b], x_send.at[0], x_recv.at[source], tensor=target
-        )
-
-    @pl.when(keeper != t)
-    def _():
-        cross(t, keeper).start()
-
-    def spread(j):
-        at = wo.at[:, place, b]
-        return remote(at, at, w_send.at[j], w_recv.at[place], dp=(z + j) % nd)
-
-    def spread_out():
-        @pl.when(keeper == t)
-        def _():
-            for j in range(1, nt):
-                cross((t + j) % nt, t).wait_recv()
-
-            def start(j, carry):
-                spread(j).start()
-                return carry
-
-            lax.fori_loop(1, nd, start, 0)
+        return exists(src, k) & (there >= 0) & (there < nd), copy
 
     def doubled(q, s, e):
         at = b
@@ -242,17 +190,88 @@
             rows, rows, d_send.at[q, index], d_recv.at[q, index], bal=flip(b, bits[ns - 1 - s])
         )
 
-    def gathered(q):
-        at = wo.at[:, q, b]
-        return remote(at, at, w_send.at[0], w_recv.at[q], dp=(z + 1) % nd)
+    def arrival(way, s, k):
+        step = 1 - 2 * way
+        src = z - step * (s + 1)
+        at = held(src, k)
+        here = remote(
+            at, at, l_send.at[way, s, k], l_recv.at[way, s, k], dp=jnp.clip(z + step, 0, nd - 1)
+        )
+        if k == groups:
+            return exists(src, k), here, doubled(jnp.clip(src, 0, nd - 1) % per, 0, 0)
+        return (
+            exists(src, k),
+            here,
+            remote(at, at, h_send.at[way, s, k], h_recv.at[way, s, k], bal=flip(b, 1)),
+        )
+
+    def begin(ks):
+        for k in ks:
+            for way in range(2):
+                valid, copy = line(way, 0, k)
+                pl.when(valid)(copy.start)
+
+    early = min(2, nd - 1)
+
+    def hop(s, k):
+        for way in range(2):
+            valid, here, half = arrival(way, s, k)
+            further, copy = line(way, s + 1, k)
+
+            @pl.when(valid)
+            def _(here=here, half=half, further=further, copy=copy):
+                here.wait_recv()
+                pl.when(further)(copy.start)
+                if part_count > 1 or k == groups:
+                    half.start()
+
+    def hops(s, ks):
+        if s < early:
+            for k in ks:
+                if k <= groups:
+                    hop(s, k)
+
+    def rest(ks):
+        for k in ks:
+            if k <= groups:
+
+                def one(s, carry, k=k):
+                    hop(s, k)
+                    return carry
+
+                lax.fori_loop(early, nd - 1, one, 0)
+
+    def halves(s, k):
+        for way in range(2):
+            valid, _, half = arrival(way, s, k)
+            if part_count > 1:
+                pl.when(valid)(half.wait_recv)
+
+    first = range(min(3, groups))
+    later = range(min(3, groups), groups)
+    begin(first)
+
+    def cross(source, target):
+        return remote(
+            wo_own.at[b], wo.at[source, place, b], x_send.at[0], x_recv.at[source], tensor=target
+        )
+
+    @pl.when(keeper != t)
+    def _():
+        cross(t, keeper).start()
+
+    def spread_out():
+        @pl.when(keeper == t)
+        def _():
+            for j in range(1, nt):
+                cross((t + j) % nt, t).wait_recv()
+            begin([groups])
+            doubled(place, 0, 0).start()
 
     def finish(s):
         def further(q, carry):
-            if s == 0:
-                pl.when(t * per + q != z)(gathered(q).wait_recv)
-            else:
-                for e in range(1 << (s - 1)):
-                    doubled(q, s - 1, e).wait_recv()
+            for e in range(1 << (s - 1)):
+                doubled(q, s - 1, e).wait_recv()
             if s < ns:
                 for e in range(1 << s):
                     doubled(q, s, e).start()
@@ -286,34 +305,10 @@
             center * lax.rsqrt(spread_of + EPSILON)
         ).astype(normed.dtype)
 
-    early = min(2, nd - 1)
-    forwards = [(s, k) for s in range(early) for k in range(groups)]
-    slots = [1, 1, 2, 2, 3, 4, 5, 5, 6, 7]
-    after = {}
-    for n, pair in enumerate(forwards):
-        after.setdefault(slots[n] if len(forwards) == len(slots) else CAP - 1, []).append(pair)
-    for p, (i, start, count) in enumerate(pieces):
-        wait_for(ns, 0, p)
-        rows = pl.ds(start, count)
-        gath[i, pl.ds(pl.multiple_of(t * slices + start, 16), count), :] = current(ns, 0, i, rows)
-        for j in range(1, nt):
-            y_copy(p, j).start()
-        if start + count == slices:
-            for s, k in after.get(i, []):
-                hop(s, k)
-            if i == 5:
-                spread_out()
-            if i >= 2:
-                normalize(i - 2)
-
-    def rest(k):
-        def one(s, carry):
-            hop(s, k)
-            return carry
-
-        lax.fori_loop(early, nd - 1, one, 0)
-
     def ready(k):
+        if k >= groups:
+            return
+
         def one(s, carry):
             halves(s, k)
             return carry
@@ -321,18 +316,18 @@
         lax.fori_loop(0, nd - 1, one, 0)
         for kind in range(kinds):
             block = wq[kind, :, :, :, k * width : (k + 1) * width].reshape(features, width)
-            wt[kind * width : (kind + 1) * width, :] = block.T
+            wt[k, kind * width : (kind + 1) * width, :] = block.T
 
     def heads_of(k):
         return [h for h in range(slices // HDIM) if k * width < (h + 1) * HDIM <= (k + 1) * width]
 
-    def c_copy(k, g, j):
+    def c_copy(k, n, j):
         first, number = heads_of(k)[0], len(heads_of(k))
         at = ctx.at[
             pl.ds(pl.multiple_of(t * slices + first * HDIM, 16), number * HDIM),
-            pl.ds(pl.multiple_of(g * GROUP * patches, patches), GROUP * patches),
+            pl.ds(pl.multiple_of(n * PAIR * patches, patches), PAIR * patches),
         ]
-        return remote(at, at, c_send.at[k, g, j], c_recv.at[k, g, j], tensor=(t + j) % nt)
+        return remote(at, at, c_send.at[k, n, j], c_recv.at[k, n, j], tensor=(t + j) % nt)
 
     def columns(i, number):
         return pl.ds(pl.multiple_of(i * patches, patches), number * patches)
@@ -340,9 +335,11 @@
     scale = HDIM ** (-0.5) * LOG2E
 
     def encode(k, g):
-        for n in range(0, GROUP, 2):
-            cols = columns(g * GROUP + n, 2)
-            result = jnp.dot(wt[...], normed[:, cols], preferred_element_type=jnp.float32)
+        if k >= groups:
+            return
+        for n in range(0, GROUP, PAIR):
+            cols = columns(g * GROUP + n, PAIR)
+            result = jnp.dot(wt[k], normed[:, cols], preferred_element_type=jnp.float32)
             for kind in range(kinds):
                 qkv[kind, k * width : (k + 1) * width, cols] = result[
                     kind * width : (kind + 1) * width
@@ -363,63 +360,83 @@
                 ctx[pl.ds(pl.multiple_of(t * slices + h * HDIM, 16), HDIM), cols] = (
                     value * (1.0 / total)
                 ).astype(ctx.dtype)
-        for j in range(1, nt):
-            c_copy(k, g, j).start()
-
-    rest(0)
-    ready(0)
-    encode(0, 0)
-    if groups > 1:
-        rest(1)
-    for i in range(CAP - 2, CAP):
-        normalize(i)
-
-    def others(k, low):
+        for n in range(GROUP // PAIR):
+            for j in range(1, nt):
+                c_copy(k, g * (GROUP // PAIR) + n, j).start()
+
+    def both(k):
+        if k >= groups:
+            return
+
         def one(g, carry):
             encode(k, g)
             return carry
 
-        lax.fori_loop(low, blocks, one, 0)
-
-    others(0, 1)
-    for k in range(1, groups):
+        lax.fori_loop(0, blocks, one, 0)
+
+    def between(i):
+        if i == 0:
+            hops(0, [0])
+        if i == 1:
+            hops(0, first[1:])
+        if i == 2:
+            hops(1, [0])
+        if i == 3:
+            hops(1, first[1:2])
+        if i == 4:
+            hops(1, first[2:])
+            begin(later)
+        if i == 5:
+            rest(first[:2])
+        if i == 6:
+            hops(0, later)
+            spread_out()
+            rest(first[2:])
+        if i >= 2:
+            normalize(i - 2)
+        if i == 6:
+            ready(0)
+            encode(0, 0)
+        if i == 7:
+            if len(first) > 1:
+                ready(1)
+                encode(1, 0)
+
+    for p, (i, start, count) in enumerate(pieces):
+        wait_for(ns, 0, p)
+        rows = pl.ds(start, count)
+        gath[i, pl.ds(pl.multiple_of(t * slices + start, 16), count), :] = current(ns, 0, i, rows)
+        for j in range(1, nt):
+            y_copy(p, j).start()
+        if start + count == slices:
+            between(i)
+
+    normalize(CAP - 2)
+    if len(first) > 2:
+        ready(2)
+        encode(2, 0)
+    hops(1, later)
+    normalize(CAP - 1)
+    for k in first:
+        encode(k, 1)
+        if k == 0:
+            hops(0, [groups])
+    for n, k in enumerate(later):
+        rest([k])
         ready(k)
-        others(k, 0)
-        if k + 1 < groups:
-            rest(k + 1)
-        if k <= ns:
-            finish(k - 1)
-    for s in range(min(groups - 1, ns), ns + 1):
+        if n == 1:
+            hops(1, [groups])
+        both(k)
+    if len(later) < 2:
+        hops(1, [groups])
+    rest([groups])
+    for s in range(1, ns + 1):
         finish(s)
 
     def partial(source, cols):
         weight = wo[source].reshape(slices, slices)
         block = ctx[pl.ds(pl.multiple_of(source * slices, 16), slices), cols]
         return jnp.dot(weight, block, preferred_element_type=jnp.float32).astype(own.dtype)
-
-    def mine(n, carry):
-        own[:, columns(2 * n, 2)] = partial(t, columns(2 * n, 2))
-        return carry
-
-    lax.fori_loop(0, CAP // 2, mine, 0)
-
-    def close(g, carry):
-        for k in range(groups):
-            for j in range(1, nt):
-                c_copy(k, g, j).wait_recv()
-        for n in range(0, GROUP, 2):
-            i = g * GROUP + n
-            total = own[:, columns(i, 2)].astype(jnp.float32)
-            for j in range(1, nt):
-                total = total + partial((t + j) % nt, columns(i, 2)).astype(jnp.float32)
-            for e in range(2):
-                source = gath[i + e, pl.ds(pl.multiple_of(t * slices, 16), slices), :]
-                out[i + e] = (
-                    source.astype(jnp.float32) + total[:, e * patches : (e + 1) * patches]
-                ).astype(out.dtype)
-        return carry
-
-    lax.fori_loop(0, blocks, close, 0)
 
     for p in range(len(pieces)):
         for j in range(1, nt):
@@ -427,22 +444,10 @@
         for s in range(ns):
             for slot in range(nb >> (s + 1)):
                 tile_copy(s, slot, p).wait_send()
-    for k in range(groups):
-        for j in range(1, nt):
-            for g in range(blocks):
-                c_copy(k, g, j).wait_send()
 
     @pl.when(keeper != t)
     def _():
         cross(t, keeper).wait_send()
-
-    @pl.when(keeper == t)
-    def _():
-        def drain(j, carry):
-            spread(j).wait_send()
-            return carry
-
-        lax.fori_loop(1, nd, drain, 0)
 
     def drain_doubled(q, carry):
         for s in range(ns):
@@ -453,16 +458,40 @@
     lax.fori_loop(0, per, drain_doubled, 0)
 
     def drain_line(s, carry):
-        for k in range(groups):
+        for k in range(groups + 1):
             for way in range(2):
                 valid, copy = line(way, s, k)
                 pl.when(valid)(copy.wait_send)
                 valid, _, half = arrival(way, s, k)
-                if part_count > 1:
+                if part_count > 1 and k < groups:
                     pl.when(valid)(half.wait_send)
         return carry
 
     lax.fori_loop(0, nd - 1, drain_line, 0)
+
+    def mine(n, carry):
+        own[:, columns(PAIR * n, PAIR)] = partial(t, columns(PAIR * n, PAIR))
+        return carry
+
+    lax.fori_loop(0, CAP // PAIR, mine, 0)
+
+    def close(n, carry):
+        for k in range(groups):
+            for j in range(1, nt):
+                c_copy(k, n, j).wait_send()
+                c_copy(k, n, j).wait_recv()
+        i = n * PAIR
+        total = own[:, columns(i, PAIR)].astype(jnp.float32)
+        for j in range(1, nt):
+            total = total + partial((t + j) % nt, columns(i, PAIR)).astype(jnp.float32)
+        for e in range(PAIR):
+            source = gath[i + e, pl.ds(pl.multiple_of(t * slices, 16), slices), :]
+            out[i + e] = (
+                source.astype(jnp.float32) + total[:, e * patches : (e + 1) * patches]
+            ).astype(out.dtype)
+        return carry
+
+    lax.fori_loop(0, CAP // PAIR, close, 0)
 
 
 def encode_all(counts, ordering, tiles, qkv_weight, out_weight):
@@ -479,7 +508,6 @@
     vmem = pl.BlockSpec(memory_space=pltpu.VMEM)
     hbm = pl.BlockSpec(memory_space=pltpu.HBM)
     dma = pltpu.SemaphoreType.DMA
-    blocks = CAP // GROUP
 
     def space(*shape):
         return pltpu.VMEM(shape, dtype)
@@ -496,7 +524,7 @@
             space(slots, slices, patches),
             space(CAP, nt * slices, patches),
             space(kinds, nd, *wq.shape[1:]),
-            space(kinds * width, nt * slices),
+            space(groups, kinds * width, nt * slices),
             space(*wo.shape),
             space(nt, per, *wo.shape),
             space(nt * slices, CAP * patches),
@@ -506,16 +534,16 @@
         ]
         + [dma((ns, max(nb // 2, 1), pieces))] * 2
         + [dma((pieces, nt))] * 2
-        + [dma((groups, blocks, nt))] * 2
-        + [dma((2, nd, groups))] * 4
-        + [dma((1,)), dma((nt,)), dma((nd,)), dma((per,))]
+        + [dma((groups, CAP // PAIR, nt))] * 2
+        + [dma((2, nd, groups + 1))] * 4
+        + [dma((1,)), dma((nt,))]
         + [dma((per, nb))] * 2
         + [dma((3,))],
         compiler_params=pltpu.CompilerParams(
             collective_id=0, has_side_effects=True, vmem_limit_bytes=44 * 1024 * 1024
         ),
         name="encode_all",
-    )(counts, ordering, tiles, wq, wo)
+    )(*(pltpu.with_memory_space_constraint(a, pltpu.HBM) for a in (counts, ordering, tiles, wq, wo)))
 
 
 def local(tiles, tile_counts, doc_order, qkv_weight, out_weight):

time: 92.2 us -> 77.5 us (0.84)
  Pallas kernels: 85.5 us -> 76.2 us
  local copies, waits for them, and re-layouts: 6.4 us -> 1.06 us
    pallas_call x1, Pallas kernels: 85.5 us -> 76.2 us  [encode_all(): pl.pallas_call(functools.partial(encode_kernel, (nd, nb, nt)), out_shape=...]
    unnamed x11 -> x1, local copies, waits for them, and re-layouts: 6.4 us -> 1.06 us
where the time goes in v2:
time: 77.5 us; the launch traced here: 77.3 us
  Pallas kernels  76.2 us (98%)
  local copies, waits for them, and re-layouts  1.06 us (1%)
    pallas_call x1, Pallas kernels, encode_all(): pl.pallas_call(functools.partial(encode_kernel, (nd, nb, nt)), out_shape=...  76.2 us

profile of v2, /device:TPU:0, one launch (start us, length us, event | category | flops | bytes accessed | tf_op | source)
XLA Modules:
  0.0 77.3 jit_solution(6628146889287994786)
XLA Ops:
  0.0 76.2 %encode_all.1 = bf16[8,640,128]{2,1,0:T(8,128)(2,1)S(1)} custom-call(s32[1,4]{1,0:T(1,128)} %refs_0_.1, s32[1,4]{1,0:T(1,128)} %refs_1_.1, bf16[16,640,128]{2,1,0:T(8,128)(2,1)} %bitcast.5, bf16[3,2,160,640]{3,2,1,0:T(8,128)(2,1)} %bitcast.6, bf16[4,80,640]{2,1,0:T(8,128)(2,1)} %bitcast.7), custom_call_target="tpu_custom_call" | custom-call | tf_op jit(solution)/shard_map/encode_all/pallas_call | solution.py:516
  76.2 1.1 %copy.7 = bf16[1,8,640,128]{3,2,1,0:T(8,128)(2,1)} copy(bf16[1,8,640,128]{3,2,1,0:T(8,128)(2,1)S(1)} %bitcast.4) | data formatting | bytes 2621440

commit v3 on v2

--- a/solution.py
+++ b/solution.py
@@ -12,6 +12,7 @@
 LANES = 128
 GROUP = 4
 PAIR = 2
+HALVES = 2
 EPSILON = 1e-06
 LOG2E = 1.4426950408889634
 MESH = pl.DeviceIdType.MESH
@@ -33,10 +34,9 @@
     return width, slices // width
 
 
-def pieces_of(slices):
-    half = slices // 2
-    first = [(0, 0, half), (0, half, half)] if half % 16 == 0 else [(0, 0, slices)]
-    return first + [(i, 0, slices) for i in range(1, CAP)]
+def pieces_of(slices, parts):
+    part = slices // parts if slices % (16 * parts) == 0 else slices
+    return [(i, start, part) for i in range(CAP) for start in range(0, slices, part)]
 
 
 def remote(src, dst, send, recv, **device):
@@ -49,28 +49,24 @@
     nd, nb, nt = sizes
     bits = bits_of(nb)
     ns = len(bits)
-    counts, order, tiles_in, wq_in, wo_in, out = refs[:6]
+    counts_in, order_in, tiles_in, wq_in, wo_in, out = refs[:6]
     sends, recvs = refs[6 : 6 + ns], refs[6 + ns : 6 + 2 * ns]
-    tiles, gath, wq, wt, wo_own, wo, normed, qkv, ctx, own = refs[6 + 2 * ns : 16 + 2 * ns]
-    sems = refs[16 + 2 * ns :]
-    t_send, t_recv, y_send, y_recv, c_send, c_recv = sems[:6]
-    l_send, l_recv, h_send, h_recv = sems[6:10]
-    x_send, x_recv, d_send, d_recv, i_sem = sems[10:]
+    tiles, gath, wq, wt, wo_own, wo, normed, qkv, ctx, own, counts, order = refs[
+        6 + 2 * ns : 18 + 2 * ns
+    ]
+    t_recv = refs[18 + 2 * ns : 18 + 3 * ns]
+    t_send, y_send, y_recv, c_send, c_recv, l_send, l_recv, h_send, h_recv = refs[
+        18 + 3 * ns : 27 + 3 * ns
+    ]
+    x_send, x_recv, d_send, d_recv, e_recv, i_sem = refs[27 + 3 * ns :]
     z, b, t = lax.axis_index("dp"), lax.axis_index("bal"), lax.axis_index("tensor")
     _, slices, patches = tiles.shape
     width, groups = column_groups(slices)
-    pieces = pieces_of(slices)
+    pieces = [pieces_of(slices, HALVES if s == ns - 1 else 1) for s in range(ns)]
     per = nd // nt
     features = nt * slices
     kinds = wq.shape[0]
     blocks = CAP // GROUP
-
-    load_tiles = pltpu.make_async_copy(tiles_in, tiles, i_sem.at[0])
-    load_q = pltpu.make_async_copy(wq_in, wq.at[:, z], i_sem.at[1])
-    load_o = pltpu.make_async_copy(wo_in, wo_own, i_sem.at[2])
-    load_tiles.start()
-    load_q.start()
-    load_o.start()
 
     barrier = pltpu.get_barrier_semaphore()
     for m in bits:
@@ -83,6 +79,19 @@
         return carry
 
     lax.fori_loop(1, nd, greet, 0)
+
+    load_counts = pltpu.make_async_copy(counts_in, counts, i_sem.at[3])
+    load_order = pltpu.make_async_copy(order_in, order, i_sem.at[4])
+    load_tiles = pltpu.make_async_copy(tiles_in, tiles, i_sem.at[0])
+    load_q = pltpu.make_async_copy(wq_in, wq.at[:, z], i_sem.at[1])
+    load_o = pltpu.make_async_copy(wo_in, wo_own, i_sem.at[2])
+    load_counts.start()
+    load_order.start()
+    load_tiles.start()
+    load_o.start()
+    load_q.start()
+    load_counts.wait()
+    load_order.wait()
 
     docs = order.shape[1]
     placed = [order[0, p] for p in range(docs)]
@@ -113,19 +122,22 @@
         return value
 
     def tile_copy(s, slot, p):
-        i, start, count = pieces[p]
+        i, start, count = pieces[s][p]
         rows = pl.ds(start, count)
         return remote(
             sends[s].at[slot, i, rows],
             recvs[s].at[slot, i, rows],
-            t_send.at[s, slot, p],
-            t_recv.at[s, slot, p],
+            t_send.at[s, slot],
+            t_recv[s].at[slot, p],
             bal=flip(b, bits[s]),
         )
 
-    def wait_for(s, r, p):
+    def wait_for(s, r, piece):
+        i, start, count = piece
         for q in range(s):
-            tile_copy(q, slot_of(q, r), p).wait_recv()
+            for p, (tile, first, number) in enumerate(pieces[q]):
+                if tile == i and start <= first < start + count:
+                    tile_copy(q, slot_of(q, r), p).wait_recv()
 
     def wanted(s):
         m = bits[s]
@@ -153,7 +165,7 @@
     pl.semaphore_wait(barrier, ns + nt - 1 + nd - 1)
 
     for r in wanted(0):
-        for p in range(len(pieces)):
+        for p in range(len(pieces[0])):
             tile_copy(0, slot_of(0, r - 1), p).start()
 
     part_count = wq.shape[2]
@@ -174,8 +186,10 @@
         src = z - step * s
         there = z + step
         at = held(src, k)
+        at_step = min(s, nd - 2) if isinstance(s, int) else jnp.minimum(s, nd - 2)
         copy = remote(
-            at, at, l_send.at[way, s, k], l_recv.at[way, s, k], dp=jnp.clip(there, 0, nd - 1)
+            at, at, l_send.at[way, at_step, int(k == groups)], l_recv.at[way, at_step, k],
+            dp=jnp.clip(there, 0, nd - 1),
         )
         return exists(src, k) & (there >= 0) & (there < nd), copy
 
@@ -185,24 +199,22 @@
             if (e >> bit) & 1:
                 at = flip(at, bits[ns - 1 - bit])
         rows = wo.at[:, q, at]
-        index = (1 << s) - 1 + e
-        return remote(
-            rows, rows, d_send.at[q, index], d_recv.at[q, index], bal=flip(b, bits[ns - 1 - s])
-        )
+        landed = e_recv.at[s] if s else d_recv.at[q]
+        return remote(rows, rows, d_send.at[0], landed, bal=flip(b, bits[ns - 1 - s]))
 
     def arrival(way, s, k):
         step = 1 - 2 * way
         src = z - step * (s + 1)
         at = held(src, k)
         here = remote(
-            at, at, l_send.at[way, s, k], l_recv.at[way, s, k], dp=jnp.clip(z + step, 0, nd - 1)
+            at, at, l_send.at[way, s, 0], l_recv.at[way, s, k], dp=jnp.clip(z + step, 0, nd - 1)
         )
         if k == groups:
             return exists(src, k), here, doubled(jnp.clip(src, 0, nd - 1) % per, 0, 0)
         return (
             exists(src, k),
             here,
-            remote(at, at, h_send.at[way, s, k], h_recv.at[way, s, k], bal=flip(b, 1)),
+            remote(at, at, h_send.at[0], h_recv.at[k], bal=flip(b, 1)),
         )
 
     def begin(ks):
@@ -213,39 +225,41 @@
 
     early = min(2, nd - 1)
 
-    def hop(s, k):
+    def hop(s, k, onward):
         for way in range(2):
             valid, here, half = arrival(way, s, k)
             further, copy = line(way, s + 1, k)
 
-            @pl.when(valid)
-            def _(here=here, half=half, further=further, copy=copy):
+            @pl.when(valid & (further if onward else jnp.logical_not(further)))
+            def _(here=here, half=half, copy=copy):
                 here.wait_recv()
-                pl.when(further)(copy.start)
+                if onward:
+                    copy.start()
                 if part_count > 1 or k == groups:
                     half.start()
 
-    def hops(s, ks):
+    def forward(s, ks):
         if s < early:
             for k in ks:
                 if k <= groups:
-                    hop(s, k)
+                    hop(s, k, True)
+
+    def accept(s, ks):
+        if s < early:
+            for k in ks:
+                if k <= groups:
+                    hop(s, k, False)
 
     def rest(ks):
         for k in ks:
             if k <= groups:
 
                 def one(s, carry, k=k):
-                    hop(s, k)
+                    hop(s, k, True)
+                    hop(s, k, False)
                     return carry
 
                 lax.fori_loop(early, nd - 1, one, 0)
-
-    def halves(s, k):
-        for way in range(2):
-            valid, _, half = arrival(way, s, k)
-            if part_count > 1:
-                pl.when(valid)(half.wait_recv)
 
     first = range(min(3, groups))
     later = range(min(3, groups), groups)
@@ -270,34 +284,37 @@
 
     def finish(s):
         def further(q, carry):
-            for e in range(1 << (s - 1)):
-                doubled(q, s - 1, e).wait_recv()
+            if s == 1:
+                doubled(q, 0, 0).wait_recv()
             if s < ns:
                 for e in range(1 << s):
                     doubled(q, s, e).start()
             return carry
 
-        lax.fori_loop(0, per, further, 0)
+        if s > 1:
+            at = wo.at[:, :, pl.ds(0, 1 << (s - 1))]
+            remote(at, at, d_send.at[0], e_recv.at[s - 1], bal=flip(b, bits[ns - s])).wait_recv()
+        if s < ns or s == 1:
+            lax.fori_loop(0, per, further, 0)
 
     for s in range(1, ns):
         for r in wanted(s):
             slot = slot_of(s, r - bits[s])
-            for p, (i, start, count) in enumerate(pieces):
-                wait_for(s, r, p)
+            for p, (i, start, count) in enumerate(pieces[s]):
+                wait_for(s, r, pieces[s][p])
                 rows = pl.ds(start, count)
                 sends[s][slot, i, rows] = current(s, r, i, rows)
                 tile_copy(s, slot, p).start()
 
-    def y_copy(p, j):
-        i, start, count = pieces[p]
+    fine = pieces[ns - 1]
+
+    def y_copy(i, start, count, j):
         at = gath.at[i, pl.ds(pl.multiple_of(t * slices + start, 16), count), :]
-        return remote(at, at, y_send.at[p, j], y_recv.at[p, j], tensor=(t + j) % nt)
+        return remote(at, at, y_send.at[j - 1], y_recv.at[i, j - 1], tensor=(t + j) % nt)
 
     def normalize(i):
-        for p, piece in enumerate(pieces):
-            if piece[0] == i:
-                for j in range(1, nt):
-                    y_copy(p, j).wait_recv()
+        for j in range(1, nt):
+            y_copy(i, 0, slices, j).wait_recv()
         values = gath[i].astype(jnp.float32)
         center = values - jnp.mean(values, axis=0, keepdims=True)
         spread_of = jnp.mean(center * center, axis=0, keepdims=True)
@@ -309,11 +326,9 @@
         if k >= groups:
             return
 
-        def one(s, carry):
-            halves(s, k)
-            return carry
-
-        lax.fori_loop(0, nd - 1, one, 0)
+        if part_count > 1:
+            at = wq.at[:, pl.ds(0, nd - 1), part, :, pl.ds(k * width, width)]
+            remote(at, at, h_send.at[0], h_recv.at[k], bal=flip(b, 1)).wait_recv()
         for kind in range(kinds):
             block = wq[kind, :, :, :, k * width : (k + 1) * width].reshape(features, width)
             wt[k, kind * width : (kind + 1) * width, :] = block.T
@@ -327,7 +342,7 @@
             pl.ds(pl.multiple_of(t * slices + first * HDIM, 16), number * HDIM),
             pl.ds(pl.multiple_of(n * PAIR * patches, patches), PAIR * patches),
         ]
-        return remote(at, at, c_send.at[k, n, j], c_recv.at[k, n, j], tensor=(t + j) % nt)
+        return remote(at, at, c_send.at[j - 1], c_recv.at[n, j - 1], tensor=(t + j) % nt)
 
     def columns(i, number):
         return pl.ds(pl.multiple_of(i * patches, patches), number * patches)
@@ -374,100 +389,104 @@
 
         lax.fori_loop(0, blocks, one, 0)
 
-    def between(i):
-        if i == 0:
-            hops(0, [0])
-        if i == 1:
-            hops(0, first[1:])
-        if i == 2:
-            hops(1, [0])
-        if i == 3:
-            hops(1, first[1:2])
-        if i == 4:
-            hops(1, first[2:])
-            begin(later)
-        if i == 5:
-            rest(first[:2])
-        if i == 6:
-            hops(0, later)
-            spread_out()
-            rest(first[2:])
-        if i >= 2:
-            normalize(i - 2)
-        if i == 6:
-            ready(0)
-            encode(0, 0)
-        if i == 7:
-            if len(first) > 1:
-                ready(1)
-                encode(1, 0)
-
-    for p, (i, start, count) in enumerate(pieces):
-        wait_for(ns, 0, p)
+    last = [groups]
+    steps = {
+        0: lambda: forward(0, [0]),
+        2: lambda: forward(0, first[1:2]),
+        3: lambda: forward(0, first[2:]),
+        5: lambda: forward(1, [0]),
+        6: lambda: forward(1, first[1:2]),
+        8: lambda: (forward(1, first[2:]), begin(later)),
+        9: lambda: (accept(0, first), accept(1, first)),
+        11: lambda: forward(0, later[:1]),
+        12: lambda: (forward(0, later[1:]), rest(first)),
+        13: spread_out,
+        14: lambda: (forward(1, later[:1]), ready(0), encode(0, 0)),
+        15: lambda: forward(1, later[1:]),
+    }
+    count_of = len(fine)
+    for p, (i, start, count) in enumerate(fine):
+        wait_for(ns, 0, (i, start, count))
         rows = pl.ds(start, count)
         gath[i, pl.ds(pl.multiple_of(t * slices + start, 16), count), :] = current(ns, 0, i, rows)
         for j in range(1, nt):
-            y_copy(p, j).start()
-        if start + count == slices:
-            between(i)
-
+            y_copy(i, start, count, j).start()
+        for at in range(2 * CAP):
+            if at * count_of // (2 * CAP) == p and at in steps:
+                steps[at]()
+        if start + count == slices and i >= 2:
+            normalize(i - 2)
+
+    ready(1)
+    encode(1, 0)
     normalize(CAP - 2)
-    if len(first) > 2:
-        ready(2)
-        encode(2, 0)
-    hops(1, later)
+    accept(0, later)
+    ready(2)
+    encode(2, 0)
+    forward(0, last)
     normalize(CAP - 1)
-    for k in first:
-        encode(k, 1)
-        if k == 0:
-            hops(0, [groups])
-    for n, k in enumerate(later):
-        rest([k])
+    encode(0, 1)
+    accept(1, later)
+    encode(1, 1)
+    forward(1, last)
+    rest(later)
+    encode(2, 1)
+    for k in later:
         ready(k)
-        if n == 1:
-            hops(1, [groups])
-        both(k)
-    if len(later) < 2:
-        hops(1, [groups])
-    rest([groups])
-    for s in range(1, ns + 1):
-        finish(s)
+        if k < groups - 1:
+            both(k)
+    if later:
+        encode(later[-1], 0)
+    accept(0, last)
+    accept(1, last)
+    rest(last)
+    if later:
+        encode(later[-1], 1)
 
     def partial(source, cols):
         weight = wo[source].reshape(slices, slices)
         block = ctx[pl.ds(pl.multiple_of(source * slices, 16), slices), cols]
         return jnp.dot(weight, block, preferred_element_type=jnp.float32).astype(own.dtype)
 
-    for p in range(len(pieces)):
-        for j in range(1, nt):
-            y_copy(p, j).wait_send()
-        for s in range(ns):
-            for slot in range(nb >> (s + 1)):
-                tile_copy(s, slot, p).wait_send()
+    for j in range(1, nt):
+        at = gath.at[:, pl.ds(0, slices), :]
+        remote(at, at, y_send.at[j - 1], y_recv.at[0, j - 1], tensor=(t + j) % nt).wait_send()
+    for s in range(ns):
+        for slot in range(nb >> (s + 1)):
+            remote(
+                sends[s].at[slot], recvs[s].at[slot], t_send.at[s, slot], t_recv[s].at[slot, 0],
+                bal=flip(b, bits[s]),
+            ).wait_send()
 
     @pl.when(keeper != t)
     def _():
         cross(t, keeper).wait_send()
 
-    def drain_doubled(q, carry):
-        for s in range(ns):
-            for e in range(1 << s):
-                doubled(q, s, e).wait_send()
+    def drain_line(s, carry):
+        for way in range(2):
+            step = 1 - 2 * way
+            src = z - step * s
+            there = z + step
+            goes = (there >= 0) & (there < nd)
+            at = wq.at[:, jnp.clip(src, 0, nd - 1), part]
+            copy = remote(
+                at, at, l_send.at[way, s, 0], l_recv.at[way, s, 0], dp=jnp.clip(there, 0, nd - 1)
+            )
+            pl.when(exists(src, 0) & goes)(copy.wait_send)
+            valid, copy = line(way, s, groups)
+            pl.when(valid)(copy.wait_send)
         return carry
 
-    lax.fori_loop(0, per, drain_doubled, 0)
-
-    def drain_line(s, carry):
-        for k in range(groups + 1):
-            for way in range(2):
-                valid, copy = line(way, s, k)
-                pl.when(valid)(copy.wait_send)
-                valid, _, half = arrival(way, s, k)
-                if part_count > 1 and k < groups:
-                    pl.when(valid)(half.wait_send)
-        return carry
-
     lax.fori_loop(0, nd - 1, drain_line, 0)
+    if part_count > 1:
+        at = wq.at[:, pl.ds(0, nd - 1), part]
+        remote(at, at, h_send.at[0], h_recv.at[0], bal=flip(b, 1)).wait_send()
+
+    for s in range(1, ns + 1):
+        finish(s)
+
+    at = wo.at[:, :, pl.ds(0, nb - 1)]
+    remote(at, at, d_send.at[0], d_recv.at[0], bal=flip(b, 1)).wait_send()
 
     def mine(n, carry):
         own[:, columns(PAIR * n, PAIR)] = partial(t, columns(PAIR * n, PAIR))
@@ -476,11 +495,11 @@
     lax.fori_loop(0, CAP // PAIR, mine, 0)
 
     def close(n, carry):
-        for k in range(groups):
-            for j in range(1, nt):
-                c_copy(k, n, j).wait_send()
-                c_copy(k, n, j).wait_recv()
         i = n * PAIR
+        for j in range(1, nt):
+            at = ctx.at[pl.ds(0, slices), columns(i, PAIR)]
+            arrived = remote(at, at, c_send.at[j - 1], c_recv.at[n, j - 1], tensor=(t + j) % nt)
+            arrived.wait_recv()
         total = own[:, columns(i, PAIR)].astype(jnp.float32)
         for j in range(1, nt):
             total = total + partial((t + j) % nt, columns(i, PAIR)).astype(jnp.float32)
@@ -492,6 +511,9 @@
         return carry
 
     lax.fori_loop(0, CAP // PAIR, close, 0)
+    for j in range(1, nt):
+        at = ctx.at[pl.ds(0, slices), :]
+        remote(at, at, c_send.at[j - 1], c_recv.at[0, j - 1], tensor=(t + j) % nt).wait_send()
 
 
 def encode_all(counts, ordering, tiles, qkv_weight, out_weight):
@@ -500,7 +522,6 @@
     slots, slices, patches = tiles.shape
     kinds, rows, columns = qkv_weight.shape
     width, groups = column_groups(columns)
-    pieces = len(pieces_of(slices))
     per = nd // nt
     wq = qkv_weight.reshape(kinds, min(nb, 2), -1, columns)
     wo = out_weight.reshape(nb, -1, columns)
@@ -516,7 +537,7 @@
     return pl.pallas_call(
         functools.partial(encode_kernel, (nd, nb, nt)),
         out_shape=jax.ShapeDtypeStruct((CAP, slices, patches), dtype),
-        in_specs=[pl.BlockSpec(memory_space=pltpu.SMEM)] * 2 + [hbm] * 3,
+        in_specs=[hbm] * 5,
         out_specs=vmem,
         scratch_shapes=buffers
         + buffers
@@ -532,13 +553,15 @@
             space(nt * slices, CAP * patches),
             space(slices, CAP * patches),
         ]
-        + [dma((ns, max(nb // 2, 1), pieces))] * 2
-        + [dma((pieces, nt))] * 2
-        + [dma((groups, CAP // PAIR, nt))] * 2
-        + [dma((2, nd, groups + 1))] * 4
-        + [dma((1,)), dma((nt,))]
-        + [dma((per, nb))] * 2
-        + [dma((3,))],
+        + [pltpu.SMEM(counts.shape, counts.dtype), pltpu.SMEM(ordering.shape, ordering.dtype)]
+        + [
+            dma((nb >> (s + 1), len(pieces_of(slices, HALVES if s == ns - 1 else 1))))
+            for s in range(ns)
+        ]
+        + [dma((ns, max(nb // 2, 1))), dma((nt - 1,)), dma((CAP, nt - 1))]
+        + [dma((nt - 1,)), dma((CAP // PAIR, nt - 1))]
+        + [dma((2, nd - 1, 2)), dma((2, nd - 1, groups + 1)), dma((1,)), dma((groups,))]
+        + [dma((1,)), dma((nt,)), dma((1,)), dma((per,)), dma((ns,)), dma((5,))],
         compiler_params=pltpu.CompilerParams(
             collective_id=0, has_side_effects=True, vmem_limit_bytes=44 * 1024 * 1024
         ),

time: 77.5 us -> 72 us (0.929)
  Pallas kernels: 76.2 us -> 70.8 us
    pallas_call x1, Pallas kernels: 76.2 us -> 70.8 us  [encode_all(): pl.pallas_call(functools.partial(encode_kernel, (nd, nb, nt)), out_shape=...]
where the time goes in v3:
time: 72 us; the launch traced here: 71.8 us
  Pallas kernels  70.8 us (98%)
  local copies, waits for them, and re-layouts  1.06 us (1%)
    pallas_call x1, Pallas kernels, encode_all(): pl.pallas_call(functools.partial(encode_kernel, (nd, nb, nt)), out_shape=...  70.8 us

profile of v3, /device:TPU:0, one launch (start us, length us, event | category | flops | bytes accessed | tf_op | source)
XLA Modules:
  0.0 71.8 jit_solution(16881076002936199625)
XLA Ops:
  0.0 70.8 %encode_all.1 = bf16[8,640,128]{2,1,0:T(8,128)(2,1)S(1)} custom-call(s32[1,4]{1,0:T(1,128)} %refs_0_.1, s32[1,4]{1,0:T(1,128)} %refs_1_.1, bf16[16,640,128]{2,1,0:T(8,128)(2,1)} %bitcast.5, bf16[3,2,160,640]{3,2,1,0:T(8,128)(2,1)} %bitcast.6, bf16[4,80,640]{2,1,0:T(8,128)(2,1)} %bitcast.7), custom_call_target="tpu_custom_call" | custom-call | tf_op jit(solution)/shard_map/encode_all/pallas_call | solution.py:537
  70.8 1.1 %copy.7 = bf16[1,8,640,128]{3,2,1,0:T(8,128)(2,1)} copy(bf16[1,8,640,128]{3,2,1,0:T(8,128)(2,1)S(1)} %bitcast.4) | data formatting | bytes 2621440

commit v4 on v3

--- a/solution.py
+++ b/solution.py
@@ -12,7 +12,7 @@
 LANES = 128
 GROUP = 4
 PAIR = 2
-HALVES = 2
+QUARTERS = 4
 EPSILON = 1e-06
 LOG2E = 1.4426950408889634
 MESH = pl.DeviceIdType.MESH
@@ -37,6 +37,15 @@
 def pieces_of(slices, parts):
     part = slices // parts if slices % (16 * parts) == 0 else slices
     return [(i, start, part) for i in range(CAP) for start in range(0, slices, part)]
+
+
+def waves_of(groups):
+    waves, start = [], 0
+    for count in (1, 2):
+        if start + count < groups:
+            waves.append((start, count))
+            start += count
+    return waves + [(start, groups - start)]
 
 
 def remote(src, dst, send, recv, **device):
@@ -62,7 +71,9 @@
     z, b, t = lax.axis_index("dp"), lax.axis_index("bal"), lax.axis_index("tensor")
     _, slices, patches = tiles.shape
     width, groups = column_groups(slices)
-    pieces = [pieces_of(slices, HALVES if s == ns - 1 else 1) for s in range(ns)]
+    waves = waves_of(groups)
+    final = len(waves)
+    pieces = [pieces_of(slices, QUARTERS if s == ns - 1 else 1) for s in range(ns)]
     per = nd // nt
     features = nt * slices
     kinds = wq.shape[0]
@@ -74,11 +85,14 @@
     for j in range(1, nt):
         pl.semaphore_signal(barrier, inc=1, device_id={"tensor": (t + j) % nt}, device_id_type=MESH)
 
-    def greet(j, carry):
-        pl.semaphore_signal(barrier, inc=1, device_id={"dp": (z + j) % nd}, device_id_type=MESH)
-        return carry
-
-    lax.fori_loop(1, nd, greet, 0)
+    for step in (-1, 1):
+
+        @pl.when((z + step >= 0) & (z + step < nd))
+        def _(step=step):
+            there = jnp.clip(z + step, 0, nd - 1)
+            pl.semaphore_signal(barrier, inc=1, device_id={"dp": there}, device_id_type=MESH)
+
+    greeted = jnp.int32(z > 0) + jnp.int32(z < nd - 1)
 
     load_counts = pltpu.make_async_copy(counts_in, counts, i_sem.at[3])
     load_order = pltpu.make_async_copy(order_in, order, i_sem.at[4])
@@ -88,8 +102,6 @@
     load_counts.start()
     load_order.start()
     load_tiles.start()
-    load_o.start()
-    load_q.start()
     load_counts.wait()
     load_order.wait()
 
@@ -144,6 +156,8 @@
         return [r for r in reversed(range(nb)) if r & (m - 1) == 0 and r & m]
 
     load_tiles.wait()
+    load_q.start()
+    load_o.start()
     for r in wanted(0):
         slot = slot_of(0, r - 1)
 
@@ -152,6 +166,12 @@
             return carry
 
         lax.fori_loop(0, CAP, fill, 0)
+
+    pl.semaphore_wait(barrier, ns + nt - 1 + greeted)
+
+    for r in wanted(0):
+        for p in range(len(pieces[0])):
+            tile_copy(0, slot_of(0, r - 1), p).start()
 
     load_o.wait()
     load_q.wait()
@@ -162,36 +182,31 @@
     def _():
         wo[t, place, b] = wo_own[b]
 
-    pl.semaphore_wait(barrier, ns + nt - 1 + nd - 1)
-
-    for r in wanted(0):
-        for p in range(len(pieces[0])):
-            tile_copy(0, slot_of(0, r - 1), p).start()
-
     part_count = wq.shape[2]
     part = b % part_count
 
-    def held(src, k):
+    def held(src, w):
         src = jnp.clip(src, 0, nd - 1)
-        if k == groups:
+        if w == final:
             return wo.at[:, src % per, b]
-        return wq.at[:, src, part, :, pl.ds(k * width, width)]
-
-    def exists(src, k):
+        start, count = waves[w]
+        return wq.at[:, src, part, :, pl.ds(start * width, count * width)]
+
+    def exists(src, w):
         valid = (src >= 0) & (src < nd)
-        return valid & (src // per == t) if k == groups else valid
-
-    def line(way, s, k):
+        return valid & (src // per == t) if w == final else valid
+
+    def line(way, s, w):
         step = 1 - 2 * way
         src = z - step * s
         there = z + step
-        at = held(src, k)
+        at = held(src, w)
         at_step = min(s, nd - 2) if isinstance(s, int) else jnp.minimum(s, nd - 2)
         copy = remote(
-            at, at, l_send.at[way, at_step, int(k == groups)], l_recv.at[way, at_step, k],
+            at, at, l_send.at[way, at_step, int(w == final)], l_recv.at[way, at_step, w],
             dp=jnp.clip(there, 0, nd - 1),
         )
-        return exists(src, k) & (there >= 0) & (there < nd), copy
+        return exists(src, w) & (there >= 0) & (there < nd), copy
 
     def doubled(q, s, e):
         at = b
@@ -202,68 +217,56 @@
         landed = e_recv.at[s] if s else d_recv.at[q]
         return remote(rows, rows, d_send.at[0], landed, bal=flip(b, bits[ns - 1 - s]))
 
-    def arrival(way, s, k):
+    def arrival(way, s, w):
         step = 1 - 2 * way
         src = z - step * (s + 1)
-        at = held(src, k)
+        at = held(src, w)
         here = remote(
-            at, at, l_send.at[way, s, 0], l_recv.at[way, s, k], dp=jnp.clip(z + step, 0, nd - 1)
+            at, at, l_send.at[way, s, 0], l_recv.at[way, s, w], dp=jnp.clip(z + step, 0, nd - 1)
         )
-        if k == groups:
-            return exists(src, k), here, doubled(jnp.clip(src, 0, nd - 1) % per, 0, 0)
-        return (
-            exists(src, k),
-            here,
-            remote(at, at, h_send.at[0], h_recv.at[k], bal=flip(b, 1)),
-        )
-
-    def begin(ks):
-        for k in ks:
-            for way in range(2):
-                valid, copy = line(way, 0, k)
-                pl.when(valid)(copy.start)
+        if w == final:
+            return exists(src, w), here, doubled(jnp.clip(src, 0, nd - 1) % per, 0, 0)
+        return exists(src, w), here, remote(at, at, h_send.at[0], h_recv.at[w], bal=flip(b, 1))
+
+    def begin(w):
+        for way in range(2):
+            valid, copy = line(way, 0, w)
+            pl.when(valid)(copy.start)
 
     early = min(2, nd - 1)
 
-    def hop(s, k, onward):
+    def hop(s, w, onward):
         for way in range(2):
-            valid, here, half = arrival(way, s, k)
-            further, copy = line(way, s + 1, k)
+            valid, here, half = arrival(way, s, w)
+            further, copy = line(way, s + 1, w)
 
             @pl.when(valid & (further if onward else jnp.logical_not(further)))
             def _(here=here, half=half, copy=copy):
                 here.wait_recv()
                 if onward:
                     copy.start()
-                if part_count > 1 or k == groups:
+                if part_count > 1 or w == final:
                     half.start()
 
-    def forward(s, ks):
-        if s < early:
-            for k in ks:
-                if k <= groups:
-                    hop(s, k, True)
-
-    def accept(s, ks):
-        if s < early:
-            for k in ks:
-                if k <= groups:
-                    hop(s, k, False)
-
-    def rest(ks):
-        for k in ks:
-            if k <= groups:
-
-                def one(s, carry, k=k):
-                    hop(s, k, True)
-                    hop(s, k, False)
-                    return carry
-
-                lax.fori_loop(early, nd - 1, one, 0)
-
-    first = range(min(3, groups))
-    later = range(min(3, groups), groups)
-    begin(first)
+    def forward(s, w):
+        if s < early and w <= final:
+            hop(s, w, True)
+
+    def accept(s, w):
+        if s < early and w <= final:
+            hop(s, w, False)
+
+    def rest(w):
+        def one(s, carry):
+            hop(s, w, True)
+            hop(s, w, False)
+            return carry
+
+        if w <= final:
+            lax.fori_loop(early, nd - 1, one, 0)
+
+    for w in range(min(2, final)):
+        begin(w)
 
     def cross(source, target):
         return remote(
@@ -279,7 +282,7 @@
         def _():
             for j in range(1, nt):
                 cross((t + j) % nt, t).wait_recv()
-            begin([groups])
+            begin(final)
             doubled(place, 0, 0).start()
 
     def finish(s):
@@ -326,9 +329,10 @@
         if k >= groups:
             return
 
-        if part_count > 1:
-            at = wq.at[:, pl.ds(0, nd - 1), part, :, pl.ds(k * width, width)]
-            remote(at, at, h_send.at[0], h_recv.at[k], bal=flip(b, 1)).wait_recv()
+        for w, (start, count) in enumerate(waves):
+            if part_count > 1 and start == k:
+                at = wq.at[:, pl.ds(0, nd - 1), part, :, pl.ds(start * width, count * width)]
+                remote(at, at, h_send.at[0], h_recv.at[w], bal=flip(b, 1)).wait_recv()
         for kind in range(kinds):
             block = wq[kind, :, :, :, k * width : (k + 1) * width].reshape(features, width)
             wt[k, kind * width : (kind + 1) * width, :] = block.T
@@ -389,20 +393,18 @@
 
         lax.fori_loop(0, blocks, one, 0)
 
-    last = [groups]
+    third = 2 if final > 2 else final + 1
     steps = {
-        0: lambda: forward(0, [0]),
-        2: lambda: forward(0, first[1:2]),
-        3: lambda: forward(0, first[2:]),
-        5: lambda: forward(1, [0]),
-        6: lambda: forward(1, first[1:2]),
-        8: lambda: (forward(1, first[2:]), begin(later)),
-        9: lambda: (accept(0, first), accept(1, first)),
-        11: lambda: forward(0, later[:1]),
-        12: lambda: (forward(0, later[1:]), rest(first)),
-        13: spread_out,
-        14: lambda: (forward(1, later[:1]), ready(0), encode(0, 0)),
-        15: lambda: forward(1, later[1:]),
+        0: lambda: forward(0, 0),
+        3: lambda: final > 1 and forward(0, 1),
+        5: lambda: forward(1, 0),
+        8: lambda: (final > 1 and forward(1, 1), final > 2 and begin(2)),
+        9: lambda: (accept(0, 0), accept(1, 0)),
+        10: lambda: final > 1 and (accept(0, 1), accept(1, 1)),
+        12: lambda: (forward(0, third), rest(0)),
+        13: lambda: final > 1 and rest(1),
+        14: lambda: (ready(0), encode(0, 0)),
+        15: lambda: (forward(1, third), spread_out()),
     }
     count_of = len(fine)
     for p, (i, start, count) in enumerate(fine):
@@ -412,7 +414,7 @@
         for j in range(1, nt):
             y_copy(i, start, count, j).start()
         for at in range(2 * CAP):
-            if at * count_of // (2 * CAP) == p and at in steps:
+            if max((at + 1) * count_of // (2 * CAP) - 1, 0) == p and at in steps:
                 steps[at]()
         if start + count == slices and i >= 2:
             normalize(i - 2)
@@ -420,26 +422,27 @@
     ready(1)
     encode(1, 0)
     normalize(CAP - 2)
-    accept(0, later)
+    accept(0, third)
     ready(2)
     encode(2, 0)
-    forward(0, last)
     normalize(CAP - 1)
     encode(0, 1)
-    accept(1, later)
+    accept(1, third)
+    forward(0, final)
     encode(1, 1)
-    forward(1, last)
-    rest(later)
     encode(2, 1)
+    rest(third)
+    later = range(3, groups)
     for k in later:
         ready(k)
         if k < groups - 1:
             both(k)
+    forward(1, final)
+    accept(0, final)
+    accept(1, final)
     if later:
         encode(later[-1], 0)
-    accept(0, last)
-    accept(1, last)
-    rest(last)
+    rest(final)
     if later:
         encode(later[-1], 1)
 
@@ -473,7 +476,7 @@
                 at, at, l_send.at[way, s, 0], l_recv.at[way, s, 0], dp=jnp.clip(there, 0, nd - 1)
             )
             pl.when(exists(src, 0) & goes)(copy.wait_send)
-            valid, copy = line(way, s, groups)
+            valid, copy = line(way, s, final)
             pl.when(valid)(copy.wait_send)
         return carry
 
@@ -484,9 +487,6 @@
 
     for s in range(1, ns + 1):
         finish(s)
-
-    at = wo.at[:, :, pl.ds(0, nb - 1)]
-    remote(at, at, d_send.at[0], d_recv.at[0], bal=flip(b, 1)).wait_send()
 
     def mine(n, carry):
         own[:, columns(PAIR * n, PAIR)] = partial(t, columns(PAIR * n, PAIR))
@@ -514,6 +514,8 @@
     for j in range(1, nt):
         at = ctx.at[pl.ds(0, slices), :]
         remote(at, at, c_send.at[j - 1], c_recv.at[0, j - 1], tensor=(t + j) % nt).wait_send()
+    at = wo.at[:, :, pl.ds(0, nb - 1)]
+    remote(at, at, d_send.at[0], d_recv.at[0], bal=flip(b, 1)).wait_send()
 
 
 def encode_all(counts, ordering, tiles, qkv_weight, out_weight):
@@ -522,6 +524,7 @@
     slots, slices, patches = tiles.shape
     kinds, rows, columns = qkv_weight.shape
     width, groups = column_groups(columns)
+    waves = len(waves_of(groups))
     per = nd // nt
     wq = qkv_weight.reshape(kinds, min(nb, 2), -1, columns)
     wo = out_weight.reshape(nb, -1, columns)
@@ -555,12 +558,12 @@
         ]
         + [pltpu.SMEM(counts.shape, counts.dtype), pltpu.SMEM(ordering.shape, ordering.dtype)]
         + [
-            dma((nb >> (s + 1), len(pieces_of(slices, HALVES if s == ns - 1 else 1))))
+            dma((nb >> (s + 1), len(pieces_of(slices, QUARTERS if s == ns - 1 else 1))))
             for s in range(ns)
         ]
         + [dma((ns, max(nb // 2, 1))), dma((nt - 1,)), dma((CAP, nt - 1))]
         + [dma((nt - 1,)), dma((CAP // PAIR, nt - 1))]
-        + [dma((2, nd - 1, 2)), dma((2, nd - 1, groups + 1)), dma((1,)), dma((groups,))]
+        + [dma((2, nd - 1, 2)), dma((2, nd - 1, waves + 1)), dma((1,)), dma((waves,))]
         + [dma((1,)), dma((nt,)), dma((1,)), dma((per,)), dma((ns,)), dma((5,))],
         compiler_params=pltpu.CompilerParams(
             collective_id=0, has_side_effects=True, vmem_limit_bytes=44 * 1024 * 1024

time: 72 us -> 69.7 us (0.968)
  Pallas kernels: 70.8 us -> 68.5 us
    pallas_call x1, Pallas kernels: 70.8 us -> 68.5 us  [encode_all(): pl.pallas_call(functools.partial(encode_kernel, (nd, nb, nt)), out_shape=...]
where the time goes in v4:
time: 69.7 us; the launch traced here: 69.5 us
  Pallas kernels  68.5 us (98%)
  local copies, waits for them, and re-layouts  1.06 us (2%)
    pallas_call x1, Pallas kernels, encode_all(): pl.pallas_call(functools.partial(encode_kernel, (nd, nb, nt)), out_shape=...  68.5 us

profile of v4, /device:TPU:0, one launch (start us, length us, event | category | flops | bytes accessed | tf_op | source)
XLA Modules:
  0.0 69.5 jit_solution(16845910975915057789)
XLA Ops:
  0.0 68.5 %encode_all.1 = bf16[8,640,128]{2,1,0:T(8,128)(2,1)S(1)} custom-call(s32[1,4]{1,0:T(1,128)} %refs_0_.1, s32[1,4]{1,0:T(1,128)} %refs_1_.1, bf16[16,640,128]{2,1,0:T(8,128)(2,1)} %bitcast.5, bf16[3,2,160,640]{3,2,1,0:T(8,128)(2,1)} %bitcast.6, bf16[4,80,640]{2,1,0:T(8,128)(2,1)} %bitcast.7), custom_call_target="tpu_custom_call" | custom-call | tf_op jit(solution)/shard_map/encode_all/pallas_call | solution.py:540
  68.5 1.1 %copy.7 = bf16[1,8,640,128]{3,2,1,0:T(8,128)(2,1)} copy(bf16[1,8,640,128]{3,2,1,0:T(8,128)(2,1)S(1)} %bitcast.4) | data formatting | bytes 2621440

commit v5 on v4

--- a/solution.py
+++ b/solution.py
@@ -39,9 +39,18 @@
     return [(i, start, part) for i in range(CAP) for start in range(0, slices, part)]
 
 
+def step_pieces(slices, last):
+    fine = pieces_of(slices, QUARTERS)
+    if last:
+        return fine
+    lead = fine[0][2]
+    first = [(0, 0, lead)] + ([(0, lead, slices - lead)] if lead < slices else [])
+    return first + [(i, 0, slices) for i in range(1, CAP)]
+
+
 def waves_of(groups):
     waves, start = [], 0
-    for count in (1, 2):
+    for count in (1, 2, 1):
         if start + count < groups:
             waves.append((start, count))
             start += count
@@ -60,20 +69,21 @@
     ns = len(bits)
     counts_in, order_in, tiles_in, wq_in, wo_in, out = refs[:6]
     sends, recvs = refs[6 : 6 + ns], refs[6 + ns : 6 + 2 * ns]
-    tiles, gath, wq, wt, wo_own, wo, normed, qkv, ctx, own, counts, order = refs[
-        6 + 2 * ns : 18 + 2 * ns
+    head, tail, gath, wq, wt, wo_own, wo, normed, qkv, ctx, own, counts, order = refs[
+        6 + 2 * ns : 19 + 2 * ns
     ]
-    t_recv = refs[18 + 2 * ns : 18 + 3 * ns]
+    t_recv = refs[19 + 2 * ns : 19 + 3 * ns]
     t_send, y_send, y_recv, c_send, c_recv, l_send, l_recv, h_send, h_recv = refs[
-        18 + 3 * ns : 27 + 3 * ns
+        19 + 3 * ns : 28 + 3 * ns
     ]
-    x_send, x_recv, d_send, d_recv, e_recv, i_sem = refs[27 + 3 * ns :]
+    x_send, x_recv, d_send, d_recv, e_recv, i_sem = refs[28 + 3 * ns :]
     z, b, t = lax.axis_index("dp"), lax.axis_index("bal"), lax.axis_index("tensor")
-    _, slices, patches = tiles.shape
+    slots, slices, patches = tiles_in.shape
+    lead = head.shape[1]
     width, groups = column_groups(slices)
     waves = waves_of(groups)
     final = len(waves)
-    pieces = [pieces_of(slices, QUARTERS if s == ns - 1 else 1) for s in range(ns)]
+    pieces = [step_pieces(slices, s == ns - 1) for s in range(ns)]
     per = nd // nt
     features = nt * slices
     kinds = wq.shape[0]
@@ -96,12 +106,18 @@
 
     load_counts = pltpu.make_async_copy(counts_in, counts, i_sem.at[3])
     load_order = pltpu.make_async_copy(order_in, order, i_sem.at[4])
-    load_tiles = pltpu.make_async_copy(tiles_in, tiles, i_sem.at[0])
+    load_head = pltpu.make_async_copy(tiles_in.at[:, pl.ds(0, lead)], head, i_sem.at[0])
+    load_tail = pltpu.make_async_copy(
+        tiles_in.at[:, pl.ds(lead, slices - lead)], tail, i_sem.at[5]
+    )
     load_q = pltpu.make_async_copy(wq_in, wq.at[:, z], i_sem.at[1])
     load_o = pltpu.make_async_copy(wo_in, wo_own, i_sem.at[2])
     load_counts.start()
     load_order.start()
-    load_tiles.start()
+    load_head.start()
+    load_tail.start()
+    load_q.start()
+    load_o.start()
     load_counts.wait()
     load_order.wait()
 
@@ -117,7 +133,8 @@
     def slot_of(s, r):
         return r >> (s + 1)
 
-    def current(s, r, i, rows):
+    def current(s, r, i, start, count):
+        rows = pl.ds(start, count)
         block = b
         for m in bits:
             if r & m:
@@ -127,7 +144,8 @@
         for p in range(docs):
             inside = (edges[p] <= packed) & (packed < edges[p + 1])
             owner = owner + jnp.where(inside, placed[p], 0)
-        value = tiles[jnp.clip(packed - own_start, 0, tiles.shape[0] - 1), rows]
+        at = jnp.clip(packed - own_start, 0, slots - 1)
+        value = head[at] if start == 0 else tail[at, pl.ds(start - lead, count)]
         for q in range(s):
             apart = (owner // bits[q]) % 2 != (b // bits[q]) % 2
             value = lax.select(apart, recvs[q][slot_of(q, r), i, rows], value)
@@ -155,23 +173,26 @@
         m = bits[s]
         return [r for r in reversed(range(nb)) if r & (m - 1) == 0 and r & m]
 
-    load_tiles.wait()
-    load_q.start()
-    load_o.start()
+    load_head.wait()
+    for r in wanted(0):
+        sends[0][slot_of(0, r - 1), 0, pl.ds(0, lead)] = current(0, r, 0, 0, lead)
+    pl.semaphore_wait(barrier, ns + nt - 1 + greeted)
+    for r in wanted(0):
+        tile_copy(0, slot_of(0, r - 1), 0).start()
+    load_tail.wait()
     for r in wanted(0):
         slot = slot_of(0, r - 1)
+        sends[0][slot, 0, pl.ds(lead, slices - lead)] = current(0, r, 0, lead, slices - lead)
+        tile_copy(0, slot, 1).start()
 
         def fill(i, carry, r=r, slot=slot):
-            sends[0][slot, i] = current(0, r, i, slice(None))
+            sends[0][slot, i, pl.ds(0, lead)] = current(0, r, i, 0, lead)
+            sends[0][slot, i, pl.ds(lead, slices - lead)] = current(0, r, i, lead, slices - lead)
             return carry
 
-        lax.fori_loop(0, CAP, fill, 0)
-
-    pl.semaphore_wait(barrier, ns + nt - 1 + greeted)
-
-    for r in wanted(0):
-        for p in range(len(pieces[0])):
-            tile_copy(0, slot_of(0, r - 1), p).start()
+        lax.fori_loop(1, CAP, fill, 0)
+        for p in range(2, len(pieces[0])):
+            tile_copy(0, slot, p).start()
 
     load_o.wait()
     load_q.wait()
@@ -214,7 +235,7 @@
             if (e >> bit) & 1:
                 at = flip(at, bits[ns - 1 - bit])
         rows = wo.at[:, q, at]
-        landed = e_recv.at[s] if s else d_recv.at[q]
+        landed = e_recv.at[s, q] if s else d_recv.at[q]
         return remote(rows, rows, d_send.at[0], landed, bal=flip(b, bits[ns - 1 - s]))
 
     def arrival(way, s, w):
@@ -285,20 +306,18 @@
             begin(final)
             doubled(place, 0, 0).start()
 
-    def finish(s):
-        def further(q, carry):
-            if s == 1:
-                doubled(q, 0, 0).wait_recv()
-            if s < ns:
-                for e in range(1 << s):
-                    doubled(q, s, e).start()
-            return carry
-
-        if s > 1:
-            at = wo.at[:, :, pl.ds(0, 1 << (s - 1))]
-            remote(at, at, d_send.at[0], e_recv.at[s - 1], bal=flip(b, bits[ns - s])).wait_recv()
-        if s < ns or s == 1:
-            lax.fori_loop(0, per, further, 0)
+    def source_of(i):
+        low = t * per
+        near = jnp.where(z < low, i, per - 1 - i)
+        return jnp.where((z >= low) & (z < low + per), (place + i) % per, near)
+
+    def complete(q):
+        doubled(q, 0, 0).wait_recv()
+        for s in range(1, ns):
+            for e in range(1 << s):
+                doubled(q, s, e).start()
+            at = wo.at[:, q, pl.ds(0, 1 << s)]
+            remote(at, at, d_send.at[0], e_recv.at[s, q], bal=flip(b, bits[ns - 1 - s])).wait_recv()
 
     for s in range(1, ns):
         for r in wanted(s):
@@ -306,7 +325,7 @@
             for p, (i, start, count) in enumerate(pieces[s]):
                 wait_for(s, r, pieces[s][p])
                 rows = pl.ds(start, count)
-                sends[s][slot, i, rows] = current(s, r, i, rows)
+                sends[s][slot, i, rows] = current(s, r, i, start, count)
                 tile_copy(s, slot, p).start()
 
     fine = pieces[ns - 1]
@@ -383,34 +402,27 @@
             for j in range(1, nt):
                 c_copy(k, g * (GROUP // PAIR) + n, j).start()
 
-    def both(k):
-        if k >= groups:
-            return
-
-        def one(g, carry):
-            encode(k, g)
-            return carry
-
-        lax.fori_loop(0, blocks, one, 0)
-
     third = 2 if final > 2 else final + 1
+    fourth = 3 if final > 3 else final + 1
     steps = {
         0: lambda: forward(0, 0),
         3: lambda: final > 1 and forward(0, 1),
         5: lambda: forward(1, 0),
-        8: lambda: (final > 1 and forward(1, 1), final > 2 and begin(2)),
+        8: lambda: (final > 1 and forward(1, 1), final > 2 and begin(2), final > 3 and begin(3)),
         9: lambda: (accept(0, 0), accept(1, 0)),
         10: lambda: final > 1 and (accept(0, 1), accept(1, 1)),
-        12: lambda: (forward(0, third), rest(0)),
+        11: lambda: forward(0, third),
+        12: lambda: (forward(0, fourth), rest(0)),
         13: lambda: final > 1 and rest(1),
-        14: lambda: (ready(0), encode(0, 0)),
-        15: lambda: (forward(1, third), spread_out()),
+        14: lambda: (forward(1, third), ready(0), encode(0, 0)),
+        15: lambda: (forward(1, fourth), spread_out()),
     }
     count_of = len(fine)
     for p, (i, start, count) in enumerate(fine):
         wait_for(ns, 0, (i, start, count))
-        rows = pl.ds(start, count)
-        gath[i, pl.ds(pl.multiple_of(t * slices + start, 16), count), :] = current(ns, 0, i, rows)
+        gath[i, pl.ds(pl.multiple_of(t * slices + start, 16), count), :] = current(
+            ns, 0, i, start, count
+        )
         for j in range(1, nt):
             y_copy(i, start, count, j).start()
         for at in range(2 * CAP):
@@ -423,20 +435,28 @@
     encode(1, 0)
     normalize(CAP - 2)
     accept(0, third)
+    accept(0, fourth)
     ready(2)
     encode(2, 0)
     normalize(CAP - 1)
     encode(0, 1)
     accept(1, third)
+    accept(1, fourth)
     forward(0, final)
     encode(1, 1)
+    rest(third)
     encode(2, 1)
-    rest(third)
     later = range(3, groups)
-    for k in later:
+    for k in later[:-1]:
         ready(k)
-        if k < groups - 1:
-            both(k)
+        encode(k, 0)
+        if k == 3:
+            rest(fourth)
+        encode(k, 1)
+    if len(later) == 1:
+        rest(fourth)
+    for k in later[-1:]:
+        ready(k)
     forward(1, final)
     accept(0, final)
     accept(1, final)
@@ -485,14 +505,24 @@
         at = wq.at[:, pl.ds(0, nd - 1), part]
         remote(at, at, h_send.at[0], h_recv.at[0], bal=flip(b, 1)).wait_send()
 
-    for s in range(1, ns + 1):
-        finish(s)
-
-    def mine(n, carry):
-        own[:, columns(PAIR * n, PAIR)] = partial(t, columns(PAIR * n, PAIR))
+    part_rows = slices // per
+
+    def mine(i, carry):
+        q = source_of(i)
+        complete(q)
+        weight = wo[t, q].reshape(part_rows, slices)
+
+        def one(n, carry):
+            block = ctx[pl.ds(pl.multiple_of(t * slices, 16), slices), columns(n * PAIR, PAIR)]
+            own[q, :, columns(n * PAIR, PAIR)] = jnp.dot(
+                weight, block, preferred_element_type=jnp.float32
+            ).astype(own.dtype)
+            return carry
+
+        lax.fori_loop(0, CAP // PAIR, one, 0)
         return carry
 
-    lax.fori_loop(0, CAP // PAIR, mine, 0)
+    lax.fori_loop(0, per, mine, 0)
 
     def close(n, carry):
         i = n * PAIR
@@ -500,7 +530,7 @@
             at = ctx.at[pl.ds(0, slices), columns(i, PAIR)]
             arrived = remote(at, at, c_send.at[j - 1], c_recv.at[n, j - 1], tensor=(t + j) % nt)
             arrived.wait_recv()
-        total = own[:, columns(i, PAIR)].astype(jnp.float32)
+        total = own[:, :, columns(i, PAIR)].reshape(slices, PAIR * patches).astype(jnp.float32)
         for j in range(1, nt):
             total = total + partial((t + j) % nt, columns(i, PAIR)).astype(jnp.float32)
         for e in range(PAIR):
@@ -525,6 +555,7 @@
     kinds, rows, columns = qkv_weight.shape
     width, groups = column_groups(columns)
     waves = len(waves_of(groups))
+    lead = pieces_of(slices, QUARTERS)[0][2]
     per = nd // nt
     wq = qkv_weight.reshape(kinds, min(nb, 2), -1, columns)
     wo = out_weight.reshape(nb, -1, columns)
@@ -545,7 +576,8 @@
         scratch_shapes=buffers
         + buffers
         + [
-            space(slots, slices, patches),
+            space(slots, lead, patches),
+            space(slots, slices - lead, patches),
             space(CAP, nt * slices, patches),
             space(kinds, nd, *wq.shape[1:]),
             space(groups, kinds * width, nt * slices),
@@ -554,17 +586,17 @@
             space(nt * slices, CAP * patches),
             space(kinds, columns, CAP * patches),
             space(nt * slices, CAP * patches),
-            space(slices, CAP * patches),
+            space(per, slices // per, CAP * patches),
         ]
         + [pltpu.SMEM(counts.shape, counts.dtype), pltpu.SMEM(ordering.shape, ordering.dtype)]
         + [
-            dma((nb >> (s + 1), len(pieces_of(slices, QUARTERS if s == ns - 1 else 1))))
+            dma((nb >> (s + 1), len(step_pieces(slices, s == ns - 1))))
             for s in range(ns)
         ]
         + [dma((ns, max(nb // 2, 1))), dma((nt - 1,)), dma((CAP, nt - 1))]
         + [dma((nt - 1,)), dma((CAP // PAIR, nt - 1))]
         + [dma((2, nd - 1, 2)), dma((2, nd - 1, waves + 1)), dma((1,)), dma((waves,))]
-        + [dma((1,)), dma((nt,)), dma((1,)), dma((per,)), dma((ns,)), dma((5,))],
+        + [dma((1,)), dma((nt,)), dma((1,)), dma((per,)), dma((ns, per)), dma((6,))],
         compiler_params=pltpu.CompilerParams(
             collective_id=0, has_side_effects=True, vmem_limit_bytes=44 * 1024 * 1024
         ),

time: 69.7 us -> 69.3 us (level)
  no operation moved by 1% of the time
where the time goes in v5:
time: 69.3 us; the launch traced here: 69.1 us
  Pallas kernels  68 us (98%)
  local copies, waits for them, and re-layouts  1.06 us (2%)
    pallas_call x1, Pallas kernels, encode_all(): pl.pallas_call(functools.partial(encode_kernel, (nd, nb, nt)), out_shape=...  68 us

profile of v5, /device:TPU:0, one launch (start us, length us, event | category | flops | bytes accessed | tf_op | source)
XLA Modules:
  0.0 69.1 jit_solution(10037387672666852722)
XLA Ops:
  0.0 68.0 %encode_all.1 = bf16[8,640,128]{2,1,0:T(8,128)(2,1)S(1)} custom-call(s32[1,4]{1,0:T(1,128)} %refs_0_.1, s32[1,4]{1,0:T(1,128)} %refs_1_.1, bf16[16,640,128]{2,1,0:T(8,128)(2,1)} %bitcast.5, bf16[3,2,160,640]{3,2,1,0:T(8,128)(2,1)} %bitcast.6, bf16[4,80,640]{2,1,0:T(8,128)(2,1)} %bitcast.7), custom_call_target="tpu_custom_call" | custom-call | tf_op jit(solution)/shard_map/encode_all/pallas_call | solution.py:571
  68.0 1.1 %copy.7 = bf16[1,8,640,128]{3,2,1,0:T(8,128)(2,1)} copy(bf16[1,8,640,128]{3,2,1,0:T(8,128)(2,1)S(1)} %bitcast.4) | data formatting | bytes 2621440

commit v6 on v5

--- a/solution.py
+++ b/solution.py
@@ -224,7 +224,7 @@
         at = held(src, w)
         at_step = min(s, nd - 2) if isinstance(s, int) else jnp.minimum(s, nd - 2)
         copy = remote(
-            at, at, l_send.at[way, at_step, int(w == final)], l_recv.at[way, at_step, w],
+            at, at, l_send.at[way, at_step, int(w == final)], l_recv.at[jnp.clip(src, 0, nd - 1), w],
             dp=jnp.clip(there, 0, nd - 1),
         )
         return exists(src, w) & (there >= 0) & (there < nd), copy
@@ -235,7 +235,7 @@
             if (e >> bit) & 1:
                 at = flip(at, bits[ns - 1 - bit])
         rows = wo.at[:, q, at]
-        landed = e_recv.at[s, q] if s else d_recv.at[q]
+        landed = e_recv.at[s - 1, q] if s else d_recv.at[q]
         return remote(rows, rows, d_send.at[0], landed, bal=flip(b, bits[ns - 1 - s]))
 
     def arrival(way, s, w):
@@ -243,7 +243,8 @@
         src = z - step * (s + 1)
         at = held(src, w)
         here = remote(
-            at, at, l_send.at[way, s, 0], l_recv.at[way, s, w], dp=jnp.clip(z + step, 0, nd - 1)
+            at, at, l_send.at[way, s, 0], l_recv.at[jnp.clip(src, 0, nd - 1), w],
+            dp=jnp.clip(z + step, 0, nd - 1),
         )
         if w == final:
             return exists(src, w), here, doubled(jnp.clip(src, 0, nd - 1) % per, 0, 0)
@@ -317,7 +318,7 @@
             for e in range(1 << s):
                 doubled(q, s, e).start()
             at = wo.at[:, q, pl.ds(0, 1 << s)]
-            remote(at, at, d_send.at[0], e_recv.at[s, q], bal=flip(b, bits[ns - 1 - s])).wait_recv()
+            remote(at, at, d_send.at[0], e_recv.at[s - 1, q], bal=flip(b, bits[ns - 1 - s])).wait_recv()
 
     for s in range(1, ns):
         for r in wanted(s):
@@ -493,7 +494,7 @@
             goes = (there >= 0) & (there < nd)
             at = wq.at[:, jnp.clip(src, 0, nd - 1), part]
             copy = remote(
-                at, at, l_send.at[way, s, 0], l_recv.at[way, s, 0], dp=jnp.clip(there, 0, nd - 1)
+                at, at, l_send.at[way, s, 0], l_recv.at[0, 0], dp=jnp.clip(there, 0, nd - 1)
             )
             pl.when(exists(src, 0) & goes)(copy.wait_send)
             valid, copy = line(way, s, final)
@@ -595,8 +596,8 @@
         ]
         + [dma((ns, max(nb // 2, 1))), dma((nt - 1,)), dma((CAP, nt - 1))]
         + [dma((nt - 1,)), dma((CAP // PAIR, nt - 1))]
-        + [dma((2, nd - 1, 2)), dma((2, nd - 1, waves + 1)), dma((1,)), dma((waves,))]
-        + [dma((1,)), dma((nt,)), dma((1,)), dma((per,)), dma((ns, per)), dma((6,))],
+        + [dma((2, nd - 1, 2)), dma((nd, waves + 1)), dma((1,)), dma((waves,))]
+        + [dma((1,)), dma((nt,)), dma((1,)), dma((per,)), dma((max(ns - 1, 1), per)), dma((6,))],
         compiler_params=pltpu.CompilerParams(
             collective_id=0, has_side_effects=True, vmem_limit_bytes=44 * 1024 * 1024
         ),

time: 69.3 us -> 69.1 us (level)
  no operation moved by 1% of the time
where the time goes in v6:
time: 69.1 us; the launch traced here: 69 us
  Pallas kernels  67.9 us (98%)
  local copies, waits for them, and re-layouts  1.06 us (2%)
    pallas_call x1, Pallas kernels, encode_all(): pl.pallas_call(functools.partial(encode_kernel, (nd, nb, nt)), out_shape=...  67.9 us

profile of v6, /device:TPU:0, one launch (start us, length us, event | category | flops | bytes accessed | tf_op | source)
XLA Modules:
  0.0 69.0 jit_solution(8214967097504957162)
XLA Ops:
  0.0 67.9 %encode_all.1 = bf16[8,640,128]{2,1,0:T(8,128)(2,1)S(1)} custom-call(s32[1,4]{1,0:T(1,128)} %refs_0_.1, s32[1,4]{1,0:T(1,128)} %refs_1_.1, bf16[16,640,128]{2,1,0:T(8,128)(2,1)} %bitcast.5, bf16[3,2,160,640]{3,2,1,0:T(8,128)(2,1)} %bitcast.6, bf16[4,80,640]{2,1,0:T(8,128)(2,1)} %bitcast.7), custom_call_target="tpu_custom_call" | custom-call | tf_op jit(solution)/shard_map/encode_all/pallas_call | solution.py:572
  67.9 1.1 %copy.7 = bf16[1,8,640,128]{3,2,1,0:T(8,128)(2,1)} copy(bf16[1,8,640,128]{3,2,1,0:T(8,128)(2,1)S(1)} %bitcast.4) | data formatting | bytes 2621440
